TPU v7x, 8 devices: a whole 2x2x1 slice. The times are simulated.
8 devices in a mesh: cp: 8 (over z, y, x, core).
Axes of the slice: x: 2, y: 2, z: 1, core: 2. Of those that a mesh axis runs over, the one named last changes fastest.
Arguments:
- queries: bfloat16 [2048, 16, 192], P('cp')
- latent: bfloat16 [2048, 512], P('cp')
- key_rope: bfloat16 [2048, 64], P('cp')
- w_uk: bfloat16 [512, 16, 128], replicated
- w_uv: bfloat16 [512, 16, 128], replicated
- d_out: bfloat16 [2048, 16, 128], P('cp')
Outputs:
- output 1: bfloat16 [2048, 16, 128], P('cp')
- output 2: bfloat16 [2048, 16, 192], P('cp')
- output 3: bfloat16 [2048, 512], P('cp')
- output 4: bfloat16 [2048, 64], P('cp')
- output 5: float32 [512, 16, 128], replicated
- output 6: float32 [512, 16, 128], replicated
All inputs are finite; a program needn't handle non-finite values.
Results may differ from a plain program's by a relative error of at most 0.0141521.
Values are sent between devices in bfloat16 or wider.
A program may use at most 1 GiB of HBM per device.

v0:
```python
import math
import jax
import jax.numpy as jnp
from jax import lax
from jax.sharding import PartitionSpec as P


def solution(mesh):
    n_dev = mesh.shape["cp"]
    seq_spec = P("cp")

    def gather_all(k_nope, values, key_rope):
        k_all = lax.all_gather(k_nope, "cp", tiled=True)
        v_all = lax.all_gather(values, "cp", tiled=True)
        r_all = lax.all_gather(key_rope, "cp", tiled=True)
        return k_all, v_all, r_all

    def local_step(queries, latent, key_rope, w_uk, w_uv, d_out):
        tok_count = queries.shape[0]
        nope_dim = w_uk.shape[-1]
        score_scale = 1.0 / math.sqrt(queries.shape[-1])
        dev_index = lax.axis_index("cp")
        q_nope = queries[:, :, :nope_dim]
        q_rope = queries[:, :, nope_dim:]
        q_pos = dev_index * tok_count + jnp.arange(tok_count)
        visible = jnp.arange(tok_count * n_dev)[None, :] <= q_pos[:, None]

        def masked_scores(k_all, r_all):
            scores = (jnp.einsum("qhd,khd->hqk", q_nope, k_all, preferred_element_type=jnp.float32)
                      + jnp.einsum("qhd,kd->hqk", q_rope, r_all, preferred_element_type=jnp.float32)) * score_scale
            return jnp.where(visible[None], scores, -1e30)

        k_nope = jnp.einsum("tl,lhd->thd", latent, w_uk, preferred_element_type=jnp.float32).astype(jnp.bfloat16)
        values = jnp.einsum("tl,lhd->thd", latent, w_uv, preferred_element_type=jnp.float32).astype(jnp.bfloat16)

        k_all, v_all, r_all = gather_all(k_nope, values, key_rope)
        scores = masked_scores(k_all, r_all)
        row_max = jnp.max(scores, axis=-1, keepdims=True)
        exp_scores = jnp.exp(scores - row_max)
        row_sum = jnp.sum(exp_scores, axis=-1, keepdims=True)
        log_norm = row_max + jnp.log(row_sum)
        fwd_prob = (exp_scores / row_sum).astype(jnp.bfloat16)
        attn_out = jnp.einsum("hqk,khd->qhd", fwd_prob, v_all, preferred_element_type=jnp.float32).astype(jnp.bfloat16)

        k_all, v_all, r_all = gather_all(k_nope, values, key_rope)
        attn_prob = jnp.exp(masked_scores(k_all, r_all) - log_norm)
        prob_b = attn_prob.astype(jnp.bfloat16)
        d_prob = jnp.einsum("qhd,khd->hqk", d_out, v_all, preferred_element_type=jnp.float32)
        row_delta = jnp.einsum("qhd,qhd->hq", d_out, attn_out, preferred_element_type=jnp.float32)[:, :, None]
        d_score = (attn_prob * (d_prob - row_delta) * score_scale).astype(jnp.bfloat16)
        d_q_nope = jnp.einsum("hqk,khd->qhd", d_score, k_all, preferred_element_type=jnp.float32)
        d_q_rope = jnp.einsum("hqk,kd->qhd", d_score, r_all, preferred_element_type=jnp.float32)
        d_query = jnp.concatenate([d_q_nope, d_q_rope], axis=-1).astype(jnp.bfloat16)
        dk_part = jnp.einsum("hqk,qhd->khd", d_score, q_nope, preferred_element_type=jnp.float32).astype(jnp.bfloat16)
        dv_part = jnp.einsum("hqk,qhd->khd", prob_b, d_out, preferred_element_type=jnp.float32).astype(jnp.bfloat16)
        dr_part = jnp.einsum("hqk,qhd->kd", d_score, q_rope, preferred_element_type=jnp.float32).astype(jnp.bfloat16)
        d_k_nope = lax.psum_scatter(dk_part, "cp", scatter_dimension=0, tiled=True)
        d_values = lax.psum_scatter(dv_part, "cp", scatter_dimension=0, tiled=True)
        d_key_rope = lax.psum_scatter(dr_part, "cp", scatter_dimension=0, tiled=True)
        d_latent = (jnp.einsum("thd,lhd->tl", d_k_nope, w_uk, preferred_element_type=jnp.float32)
                    + jnp.einsum("thd,lhd->tl", d_values, w_uv, preferred_element_type=jnp.float32)).astype(jnp.bfloat16)
        d_w_uk = lax.psum(jnp.einsum("tl,thd->lhd", latent, d_k_nope, preferred_element_type=jnp.float32), "cp")
        d_w_uv = lax.psum(jnp.einsum("tl,thd->lhd", latent, d_values, preferred_element_type=jnp.float32), "cp")
        return attn_out, d_query, d_latent, d_key_rope, d_w_uk, d_w_uv

    return jax.shard_map(local_step, mesh=mesh,
                         in_specs=(seq_spec, seq_spec, seq_spec, P(), P(), seq_spec),
                         out_specs=(seq_spec, seq_spec, seq_spec, seq_spec, P(), P()),
                         check_vma=False)
```

profile of v0, /device:TPU:0, one launch (start us, length us, event | category | flops | bytes accessed | tf_op | source)
XLA Modules:
  0.0 455.7 jit_solution(8387083558624938267)
XLA Ops:
  7.2 0.0 copy-start
  7.2 0.0 all-gather.5.cloned.1.call-start
  7.2 3.5 fusion.24
  10.7 0.0 all-gather.5.cloned.1.call-update
  10.8 0.0 all-gather.3.cloned.1.call-start
  10.8 2.7 fusion.21
  13.5 0.0 all-gather.3.cloned.1.call-update
  13.5 0.0 reduce-scatter.4.cloned.1.call-start
  13.6 0.0 copy-done.3
  13.6 16.9 %all_gather.14 = bf16[2048,64]{0,1:T(8,128)(2,1)S(1)} all-gather(bf16[256,64]{0,1:T(8,128)(2,1)S(1)} %copy-done.3), channel_id=1, replica_groups=mesh['cp'=8] {'cp'}, dimensions={0}, use_global_device_ids=true | all-gather | bytes 294912 | tf_op jit(solution)/shard_map/all_gather | solution.py:15
  30.4 0.3 iota_compare_fusion
  30.8 32.5 %all-gather.5.cloned.1.call-done = bf16[2048,16,128]{2,0,1:T(8,128)(2,1)} async-done(((bf16[256,16,128]{2,0,1:T(8,128)(2,1)}), bf16[2048,16,128]{2,0,1:T(8,128)(2,1)}) %all-gather.5.cloned.1.call-update) | async-done | bytes 8388624 | tf_op jit(solution)/shard_map/all_gather | solution.py:13
  63.3 19.2 %fusion.44 = f32[16,2048,256]{2,1,0:T(8,128)} fusion(bf16[2048,16,128]{2,0,1:T(8,128)(2,1)} %all-gather.5.cloned.1.call-done, bf16[256,16,192]{0,2,1:T(8,128)(2,1)} %param.6), kind=kOutput, calls=%fused_computation.45 | convolution fusion | flops 2147483648 | bytes 42991616 | tf_op jit(solution)/shard_map/qhd,khd->hqk/dot_general | solution.py:29
  82.5 22.0 %fusion.55 = (f32[16,256]{1,0:T(8,128)S(1)}, f32[16,256,2048]{1,2,0:T(8,128)}) fusion(bf16[256,16,192]{0,2,1:T(8,128)(2,1)} %param.6, bf16[2048,64]{0,1:T(8,128)(2,1)S(1)} %all_gather.14, f32[16,2048,256]{2,1,0:T(8,128)} %fusion.44, pred[256,2048]{0,1:T(8,128)(4,1)S(1)} %iota_compare_fusion), kind=kOutput, calls=%fused_computation.58 | convolution fusion | flops 1107292160 | bytes 68435968 | tf_op jit(solution)/shard_map/qhd,kd->hqk/dot_general | solution.py:30
  104.5 13.1 %fusion.4 = f32[16,256]{1,0:T(8,128)S(1)} fusion(f32[16,256,2048]{1,2,0:T(8,128)} %get-tuple-element.15, f32[16,256]{1,0:T(8,128)S(1)} %get-tuple-element.14), kind=kLoop, calls=%fused_computation.9 | loop fusion | flops 16773120 | bytes 33587200 | tf_op jit(solution)/shard_map/reduce_sum | solution.py:40
  117.6 0.0 copy-start.1
  117.7 0.0 all-gather.3.cloned.1.call-done
  117.7 18.2 %bitcast_convert_fusion = (f32[16,256,128]{1,2,0:T(8,128)}, bf16[16,128,256]{2,1,0:T(8,128)(2,1)}) fusion(bf16[2048,16,128]{2,0,1:T(8,128)(2,1)} %all-gather.3.cloned.1.call-done, f32[16,256,2048]{1,2,0:T(8,128)} %get-tuple-element.15, f32[16,256]{1,0:T(8,128)S(1)} %fusion.4, f32[16,256]{1,0:T(8,128)S(1)} %get-tuple-element.14), kind=kOutput, calls=%fused_computation.42 | convolution fusion | flops 2173698048 | bytes 45121536 | tf_op jit(solution)/shard_map/hqk,khd->qhd/dot_general | solution.py:43
  135.9 3.0 copy.37
  138.9 0.0 copy-done.1
  138.9 2.2 multiply_reduce_fusion
  141.1 0.7 copy.38
  141.8 21.0 %fusion.1 = bf16[16,256,2048]{1,2,0:T(8,128)(2,1)} fusion(f32[16,256,2048]{1,2,0:T(8,128)} %get-tuple-element.15, f32[16,256]{1,0:T(8,128)} %copy.38, f32[16,256]{1,0:T(8,128)S(1)} %log_add_fusion, bf16[2048,16,128]{2,0,1:T(8,128)(2,1)} %all-gather.3.cloned.1.call-done, bf16[256,16,128]{2,1,0:T(8,128)(2,1)S(1)} %copy-done.1), kind=kOutput, calls=%fused_computation.2 | convolution fusion | flops 2189426688 | bytes 59801600 | tf_op jit(solution)/shard_map/qhd,khd->hqk/dot_general | solution.py:48
  162.8 10.4 %convert_bitcast_fusion.1 = bf16[2048,16,128]{2,0,1:T(8,128)(2,1)} fusion(bf16[16,256,2048]{1,2,0:T(8,128)(2,1)} %fusion.1, bf16[256,16,192]{0,2,1:T(8,128)(2,1)} %param.6), kind=kOutput, calls=%fused_computation.15 | convolution fusion | flops 2151677952 | bytes 26214400 | tf_op jit(solution)/shard_map/hqk,qhd->khd/dot_general | solution.py:54
  173.2 0.0 reduce-scatter.4.cloned.1.call-update
  173.2 0.0 reduce-scatter.6.cloned.1.call-start
  173.3 16.7 %convert_bitcast_fusion = bf16[2048,16,128]{2,0,1:T(8,128)(2,1)} fusion(f32[16,256,2048]{1,2,0:T(8,128)} %get-tuple-element.15, f32[16,256]{1,0:T(8,128)S(1)} %log_add_fusion, bf16[256,16,128]{2,1,0:T(8,128)(2,1)S(1)} %copy-done.1), kind=kOutput, calls=%fused_computation.14 | convolution fusion | flops 2168455168 | bytes 43008000 | tf_op jit(solution)/shard_map/hqk,qhd->khd/dot_general | solution.py:55
  190.0 0.0 reduce-scatter.6.cloned.1.call-update
  190.0 0.0 copy-start.2
  190.1 0.0 all-reduce.3.cloned.1.call-start
  190.1 45.5 %reduce-scatter.4.cloned.1.call-done = bf16[256,16,128]{2,0,1:T(8,128)(2,1)} async-done(((bf16[2048,16,128]{2,0,1:T(8,128)(2,1)}), bf16[256,16,128]{2,0,1:T(8,128)(2,1)}) %reduce-scatter.4.cloned.1.call-update) | async-done | bytes 1048592 | tf_op jit(solution)/shard_map/reduce_scatter | solution.py:57
  235.6 4.0 convolution_bitcast_fusion.2
  239.7 61.5 %reduce-scatter.6.cloned.1.call-done = bf16[256,16,128]{2,0,1:T(8,128)(2,1)} async-done(((bf16[2048,16,128]{2,0,1:T(8,128)(2,1)}), bf16[256,16,128]{2,0,1:T(8,128)(2,1)}) %reduce-scatter.6.cloned.1.call-update) | async-done | bytes 1048592 | tf_op jit(solution)/shard_map/reduce_scatter | solution.py:58
  301.2 4.0 convolution_bitcast_fusion.1
  305.2 0.0 all-reduce.3.cloned.1.call-update
  305.2 0.0 reduce-scatter.8.cloned.1.call-start
  305.3 1.8 copy.27
  307.1 9.6 %fusion.29 = bf16[256,16,64]{0,2,1:T(8,128)(2,1)} fusion(bf16[16,256,2048]{1,2,0:T(8,128)(2,1)} %fusion.1, bf16[2048,64]{0,1:T(8,128)(2,1)S(1)} %all_gather.14), kind=kOutput, calls=%fused_computation.37 | convolution fusion | flops 1074003968 | bytes 17563648 | tf_op jit(solution)/shard_map/hqk,kd->qhd/dot_general | solution.py:52
  316.6 11.7 %fusion.12 = bf16[2048,64]{0,1:T(8,128)(2,1)} fusion(bf16[16,256,2048]{1,2,0:T(8,128)(2,1)} %fusion.1, bf16[256,16,192]{0,2,1:T(8,128)(2,1)} %param.6), kind=kOutput, calls=%fused_computation.17 | convolution fusion | flops 1073872896 | bytes 17563648 | tf_op jit(solution)/shard_map/hqk,qhd->kd/dot_general | solution.py:56
  328.3 0.0 reduce-scatter.8.cloned.1.call-update
  328.3 11.1 %fusion.28 = bf16[256,16,128]{0,2,1:T(8,128)(2,1)S(1)} fusion(bf16[2048,16,128]{2,0,1:T(8,128)(2,1)} %all-gather.5.cloned.1.call-done, bf16[16,256,2048]{1,2,0:T(8,128)(2,1)} %fusion.1), kind=kOutput, calls=%fused_computation.35 | convolution fusion | flops 2148007936 | bytes 26214400 | tf_op jit(solution)/shard_map/hqk,khd->qhd/dot_general | solution.py:51
  339.4 2.3 pad_maximum_fusion
  341.8 2.0 fusion.30
  343.7 3.4 fusion.39
  347.1 72.9 %all-reduce.3.cloned.1.call-done = (f32[512,16,128]{0,2,1:T(8,128)}, f32[512,16,128]{0,2,1:T(8,128)}) async-done(((f32[512,16,128]{0,2,1:T(8,128)}, f32[512,16,128]{0,2,1:T(8,128)}), (f32[512,16,128]{0,2,1:T(8,128)}, f32[512,16,128]{0,2,1:T(8,128)})) %all-reduce.3.cloned.1.call-update) | async-done | bytes 8388624 | tf_op jit(solution)/shard_map/psum | solution.py:62
  420.0 5.4 %copy.28 = f32[512,16,128]{2,1,0:T(8,128)} copy(f32[512,16,128]{0,2,1:T(8,128)} %get-tuple-element.12) | data formatting | bytes 8388608
  425.4 5.4 %copy.29 = f32[512,16,128]{2,1,0:T(8,128)} copy(f32[512,16,128]{0,2,1:T(8,128)} %get-tuple-element.13) | data formatting | bytes 8388608
  430.9 18.0 %reduce-scatter.8.cloned.1.call-done = bf16[256,64]{0,1:T(8,128)(2,1)} async-done(((bf16[2048,64]{0,1:T(8,128)(2,1)}), bf16[256,64]{0,1:T(8,128)(2,1)}) %reduce-scatter.8.cloned.1.call-update) | async-done | bytes 32784 | tf_op jit(solution)/shard_map/reduce_scatter | solution.py:59
  (5 shorter events, 0.0 us)
Async XLA Ops:
  7.2 3.7 copy-start
  7.2 6.4 %copy-start.3 = (bf16[256,64]{0,1:T(8,128)(2,1)S(1)}, bf16[256,64]{0,1:T(8,128)(2,1)}, u32[]{:S(2)}) copy-start(bf16[256,64]{0,1:T(8,128)(2,1)} %param.8) | copy-start | bytes 98308
  7.2 56.1 %all-gather.5.cloned.1.call-start = ((), (), s32[]{:S(2)}) async-start(), calls=%async_computation.4 | async-start | bytes 9437184 | tf_op jit(solution)/shard_map/all_gather | solution.py:13
  10.8 106.9 %all-gather.3.cloned.1.call-start = ((), (), s32[]{:S(2)}) async-start(), calls=%async_computation.3 | async-start | bytes 9437184 | tf_op jit(solution)/shard_map/all_gather | solution.py:14
  13.5 222.1 %reduce-scatter.4.cloned.1.call-start = ((), (), s32[]{:S(2)}) async-start(), calls=%async_computation.5 | async-start | bytes 9437184 | tf_op jit(solution)/shard_map/reduce_scatter | solution.py:57
  117.6 21.3 %copy-start.1 = (bf16[256,16,128]{2,1,0:T(8,128)(2,1)S(1)}, bf16[256,16,128]{2,1,0:T(8,128)(2,1)}, u32[]{:S(2)}) copy-start(bf16[256,16,128]{2,1,0:T(8,128)(2,1)} %param.11) | copy-start | bytes 3145732
  173.2 127.9 %reduce-scatter.6.cloned.1.call-start = ((), (), s32[]{:S(2)}) async-start(), calls=%async_computation.6 | async-start | bytes 9437184 | tf_op jit(solution)/shard_map/reduce_scatter | solution.py:58
  190.0 115.2 %copy-start.2 = (bf16[16,128,256]{2,1,0:T(8,128)(2,1)S(1)}, bf16[16,128,256]{2,1,0:T(8,128)(2,1)}, u32[]{:S(2)}) copy-start(bf16[16,128,256]{2,1,0:T(8,128)(2,1)} %get-tuple-element.17) | copy-start | bytes 3145732
  190.1 230.0 %all-reduce.3.cloned.1.call-start = ((), (), s32[]{:S(2)}) async-start(), calls=%async_computation.8 | async-start | bytes 16777216 | tf_op jit(solution)/shard_map/psum | solution.py:62
  305.2 143.7 %reduce-scatter.8.cloned.1.call-start = ((), (), s32[]{:S(2)}) async-start(), calls=%async_computation.7 | async-start | bytes 294912 | tf_op jit(solution)/shard_map/reduce_scatter | solution.py:59
Sparse Core Ops, SparseCore 0:
  10.9 52.3 all-gather.4
  65.7 48.3 all-gather.2
  173.3 62.2 reduce-scatter.3
  238.9 62.2 reduce-scatter.5
  305.3 114.6 all-reduce.2
  423.4 25.4 reduce-scatter.7
where the time goes:
time: 456 us
  waiting for transfers between devices  231 us (51%)
  matrix products  159 us (35%)
  other arithmetic  17.9 us (4%)
  blocking collectives  16.9 us (4%)
  local copies, waits for them, and re-layouts  16.4 us (4%)
  between operations  14.2 us (3%)
    psum x1, waiting for transfers between devices, local_step(): lax.psum(jnp.einsum('tl,thd->lhd', latent, d_k_nope, preferred_element_ty...  72.9 us
    reduce_scatter x1, waiting for transfers between devices, local_step(): d_values = lax.psum_scatter(dv_part, 'cp', scatter_dimension=0, tiled=True)  61.5 us
    reduce_scatter x1, waiting for transfers between devices, local_step(): d_k_nope = lax.psum_scatter(dk_part, 'cp', scatter_dimension=0, tiled=True)  45.5 us
    all_gather x1, waiting for transfers between devices, gather_all(): k_all = lax.all_gather(k_nope, 'cp', tiled=True)  32.5 us
    dot_general x1, matrix products, masked_scores(): jnp.einsum('qhd,kd->hqk', q_rope, r_all, preferred_element_type=jnp.float32)  22 us
    dot_general x1, matrix products, local_step(): jnp.einsum('qhd,khd->hqk', d_out, v_all, preferred_element_type=jnp.float32)  21 us
    dot_general x1, matrix products, masked_scores(): jnp.einsum('qhd,khd->hqk', q_nope, k_all, preferred_element_type=jnp.floa...  19.2 us
    dot_general x1, matrix products, local_step(): jnp.einsum('hqk,khd->qhd', fwd_prob, v_all, preferred_element_type=jnp.fl...  18.2 us
  transfers between devices with their start and end apart: 6, of which 5 were waited for; matrix products, arithmetic and copies ran while one was open for 29% of the time, Pallas kernels for 0%

commit v1 on v0

v1 whole, which is shorter than its diff:
```python
import functools
import math
import jax
import jax.numpy as jnp
from jax import lax
from jax.experimental import pallas as pl
from jax.experimental.pallas import tpu as pltpu
from jax.sharding import PartitionSpec as P

F32 = jnp.float32
BF16 = jnp.bfloat16
TOK = 256
CH = 512
HPC = 8
NOPE = 128
ROPE = 64
LAT = 512
NCHIP = 4
PAIRS = [[2 * i, 2 * i + 1] for i in range(4)]
CHIPS = [[0, 2, 4, 6], [1, 3, 5, 7]]


def nt(a, b):
    return lax.dot_general(a, b, (((1,), (1,)), ((), ())), preferred_element_type=F32)


def nn(a, b):
    return lax.dot_general(a, b, (((1,), (0,)), ((), ())), preferred_element_type=F32)


def tn(a, b):
    return lax.dot_general(a, b, (((0,), (0,)), ((), ())), preferred_element_type=F32)


def attn_kernel(q_ref, do_ref, c_ref, r_ref, w_ref, o_ref, dq_ref, dw_ref, dc_ref, dr_ref,
                ct, kv, qt, dot_, s_buf, p_buf):
    scale = 1.0 / math.sqrt(NOPE + ROPE)
    c2 = scale * math.log2(math.e)
    chip = lax.axis_index("cp") // 2

    dc_ref[...] = jnp.zeros_like(dc_ref)
    dr_ref[...] = jnp.zeros_like(dr_ref)

    def tr_chunk(j, _):
        rows = pl.ds(pl.multiple_of(j * CH, CH), CH)
        ct[j] = c_ref[rows, :].T
        return 0
    lax.fori_loop(0, chip + 1, tr_chunk, 0)

    def step(s, _):
        dw_ref[s] = jnp.zeros((LAT, 4 * NOPE), F32)
        for a in range(2):
            h = 2 * s + a
            qt[a] = q_ref[h].T
            dot_[a] = do_ref[h].T

        def phase1(j, stats, masked):
            rows = pl.ds(pl.multiple_of(j * CH, CH), CH)
            kvv = nn(c_ref[rows, :], w_ref[s]).astype(BF16)
            kv[rows, :] = kvv
            rp = r_ref[rows, :]
            out = []
            for a in range(2):
                k_cat = jnp.concatenate([kvv[:, a * NOPE:(a + 1) * NOPE], rp], axis=1)
                s2 = nn(k_cat, qt[a]) * c2
                if masked:
                    ki = lax.broadcasted_iota(jnp.int32, (CH, CH), 0)
                    qi = lax.broadcasted_iota(jnp.int32, (CH, CH), 1)
                    s2 = jnp.where(ki <= qi, s2, -1e30)
                s_buf[a, rows, :] = s2
                cm = jnp.max(s2, axis=0, keepdims=True)
                if stats is None:
                    m = cm
                    l = jnp.sum(jnp.exp2(s2 - m), axis=0, keepdims=True)
                else:
                    m0, l0 = stats[a]
                    m = jnp.maximum(m0, cm)
                    l = l0 * jnp.exp2(m0 - m) + jnp.sum(jnp.exp2(s2 - m), axis=0, keepdims=True)
                out.append((m, l))
            return tuple(out)

        stats = phase1(chip, None, True)
        stats = lax.fori_loop(0, chip, lambda j, st: phase1(j, st, False), stats)
        lse = [m + jnp.log2(l) for m, l in stats]

        def phase2(j, acc):
            rows = pl.ds(pl.multiple_of(j * CH, CH), CH)
            out = []
            for a in range(2):
                pb = jnp.exp2(s_buf[a, rows, :] - lse[a]).astype(BF16)
                p_buf[a, rows, :] = pb
                v = kv[rows, (2 + a) * NOPE:(3 + a) * NOPE]
                out.append(acc[a] + tn(v, pb))
            return tuple(out)

        ot = lax.fori_loop(0, chip + 1, phase2, tuple(jnp.zeros((NOPE, CH), F32) for _ in range(2)))
        delta = []
        for a in range(2):
            h = 2 * s + a
            delta.append(jnp.sum(ot[a] * dot_[a].astype(F32), axis=0, keepdims=True))
            o_ref[h] = ot[a].T.astype(BF16)

        def phase3(j, acc):
            rows = pl.ds(pl.multiple_of(j * CH, CH), CH)
            dks, dvs, out = [], [], []
            rp = r_ref[rows, :]
            dr = jnp.zeros((CH, NOPE), F32)
            for a in range(2):
                h = 2 * s + a
                k = kv[rows, a * NOPE:(a + 1) * NOPE]
                v = kv[rows, (2 + a) * NOPE:(3 + a) * NOPE]
                pb = p_buf[a, rows, :]
                dp = nn(v, dot_[a])
                ds = (pb.astype(F32) * (dp - delta[a])).astype(BF16)
                k_cat = jnp.concatenate([k, rp], axis=1)
                out.append(acc[a] + tn(k_cat, ds))
                dkr = nn(ds, q_ref[h]) * scale
                dks.append(dkr[:, :NOPE].astype(BF16))
                dr = dr + dkr[:, NOPE:]
                dvs.append(nn(pb, do_ref[h]).astype(BF16))
            dkv = jnp.concatenate(dks + dvs, axis=1)
            dr_ref[rows, :] += dr
            dc_ref[rows, :] += nt(dkv, w_ref[s])
            dw_ref[s] += nn(ct[j], dkv)
            return tuple(out)

        dqt = lax.fori_loop(0, chip + 1, phase3, tuple(jnp.zeros((2 * NOPE, CH), F32) for _ in range(2)))
        for a in range(2):
            dq_ref[2 * s + a] = (dqt[a].T * scale).astype(BF16)
        return 0

    lax.fori_loop(0, HPC // 2, step, 0)


def solution(mesh):
    seq_spec = P("cp")

    def local_step(queries, latent, key_rope, w_uk, w_uv, d_out):
        me = lax.axis_index("cp")
        core = me % 2
        swap = [(i, i ^ 1) for i in range(8)]

        def heads_of_core(x):
            xt = jnp.transpose(x, (1, 0, 2))
            mine = lax.dynamic_slice_in_dim(xt, core * HPC, HPC, axis=0)
            other = lax.dynamic_slice_in_dim(xt, (1 - core) * HPC, HPC, axis=0)
            got = lax.ppermute(other, "cp", swap)
            first = jnp.where(core == 0, mine, got)
            second = jnp.where(core == 0, got, mine)
            return jnp.concatenate([first, second], axis=1)

        def tokens_of_core(x):
            mine = lax.dynamic_slice_in_dim(x, core * TOK, TOK, axis=1)
            other = lax.dynamic_slice_in_dim(x, (1 - core) * TOK, TOK, axis=1)
            got = lax.ppermute(other, "cp", swap)
            lo = jnp.where(core == 0, mine, got)
            hi = jnp.where(core == 0, got, mine)
            return jnp.transpose(jnp.concatenate([lo, hi], axis=0), (1, 0, 2))

        q2 = heads_of_core(jnp.pad(queries, ((0, 0), (0, 0), (0, 64))))
        do2 = heads_of_core(d_out)
        cr = jnp.concatenate([latent, key_rope, jnp.zeros((TOK, 64), BF16)], axis=1)
        cr_all = lax.all_gather(cr, "cp", tiled=True)
        c_all, r_all = cr_all[:, :LAT], cr_all[:, LAT:]

        def w_half(w):
            w = lax.dynamic_slice_in_dim(w, core * HPC, HPC, axis=1)
            return jnp.transpose(w.reshape(LAT, 4, 2 * NOPE), (1, 0, 2))
        wcat = jnp.concatenate([w_half(w_uk), w_half(w_uv)], axis=2)

        n = CH * NCHIP
        o2, dq2, dw, dc, dr = pl.pallas_call(
            attn_kernel,
            out_shape=(jax.ShapeDtypeStruct((HPC, CH, NOPE), BF16),
                       jax.ShapeDtypeStruct((HPC, CH, 2 * NOPE), BF16),
                       jax.ShapeDtypeStruct((4, LAT, 4 * NOPE), F32),
                       jax.ShapeDtypeStruct((n, LAT), F32),
                       jax.ShapeDtypeStruct((n, NOPE), F32)),
            in_specs=[pl.BlockSpec(memory_space=pltpu.VMEM)] * 5,
            out_specs=[pl.BlockSpec(memory_space=pltpu.VMEM)] * 5,
            scratch_shapes=[pltpu.VMEM((NCHIP, LAT, CH), BF16),
                            pltpu.VMEM((n, 4 * NOPE), BF16),
                            pltpu.VMEM((2, 2 * NOPE, CH), BF16),
                            pltpu.VMEM((2, NOPE, CH), BF16),
                            pltpu.VMEM((2, n, CH), F32),
                            pltpu.VMEM((2, n, CH), BF16)],
            compiler_params=pltpu.CompilerParams(vmem_limit_bytes=62 << 20),
            cost_estimate=pl.CostEstimate(flops=30 * 10**9, bytes_accessed=20 << 20, transcendentals=10**7),
        )(q2, do2, c_all, r_all, wcat)

        attn_out = tokens_of_core(o2)
        d_query = tokens_of_core(dq2)[:, :, :NOPE + ROPE]
        d_latent = lax.psum_scatter(dc, "cp", scatter_dimension=0, tiled=True).astype(BF16)
        d_key_rope = lax.psum_scatter(dr[:, :ROPE], "cp", scatter_dimension=0, tiled=True).astype(BF16)

        dw = lax.psum(dw, "cp", axis_index_groups=CHIPS)
        dw = lax.all_gather(dw, "cp", axis_index_groups=PAIRS)
        dw = dw.reshape(2, 4, LAT, 2, 2, NOPE)
        dw = jnp.transpose(dw, (3, 2, 0, 1, 4, 5)).reshape(2, LAT, 16, NOPE)
        return attn_out, d_query, d_latent, d_key_rope, dw[0], dw[1]

    return jax.shard_map(local_step, mesh=mesh,
                         in_specs=(seq_spec, seq_spec, seq_spec, P(), P(), seq_spec),
                         out_specs=(seq_spec, seq_spec, seq_spec, seq_spec, P(), P()),
                         check_vma=False)
```

time: 456 us -> 335 us (0.73)
  matrix products: 159 us -> 0 us
  local copies, waits for them, and re-layouts: 16.4 us -> 57.4 us
  Pallas kernels: 0 us -> 25.7 us
  blocking collectives: 16.9 us -> 0 us
  waiting for transfers between devices: 231 us -> 220 us
    dot_general x15 -> x0, matrix products: 159 us -> none  [the longest x1 22 us: masked_scores(): jnp.einsum('qhd,kd->hqk', q_rope, r_all, preferred_element_type=jnp.float32)]
    psum x1, waiting for transfers between devices: 72.9 us -> 136 us  [local_step(): dw = lax.psum(dw, 'cp', axis_index_groups=CHIPS)]
    reduce_scatter x3 -> x2, waiting for transfers between devices: 125 us -> 62.6 us  [the longest x1 41.7 us: local_step(): lax.psum_scatter(dc, 'cp', scatter_dimension=0, tiled=True).astype(BF16)]
    pallas_call x0 -> x1, Pallas kernels: none -> 25.7 us  [local_step(): pl.pallas_call(attn_kernel, out_shape=(jax.ShapeDtypeStruct((HPC, CH, NOP...]
    slice x0 -> x5, local copies, waits for them, and re-layouts: none -> 20.1 us  [the longest x3 15.1 us: local_step(): return (attn_out, d_query, d_latent, d_key_rope, dw[0], dw[1])]
    all_gather x1 -> x0, blocking collectives: 16.9 us -> none  [gather_all(): r_all = lax.all_gather(key_rope, 'cp', tiled=True)]
    reshape x0 -> x3, local copies, waits for them, and re-layouts: none -> 15.1 us  [the longest x1 10.5 us: local_step(): dw = dw.reshape(2, 4, LAT, 2, 2, NOPE)]
    all_gather x2, waiting for transfers between devices: 32.6 us -> 18.6 us  [the longest x1 17.6 us: local_step(): dw = lax.all_gather(dw, 'cp', axis_index_groups=PAIRS)]
  transfers between devices with their start and end apart: 6 -> 9, of which waited for: 5 -> 6; matrix products, arithmetic and copies ran while one was open for 29% -> 11% of each run, Pallas kernels for 0% -> 0%
where the time goes in v1:
time: 335 us; the launch traced here: 334 us
  waiting for transfers between devices  220 us (66%)
  local copies, waits for them, and re-layouts  57.4 us (17%)
  Pallas kernels  25.7 us (8%)
  other arithmetic  14.7 us (4%)
  between operations  13.9 us (4%)
    psum x1, waiting for transfers between devices, local_step(): dw = lax.psum(dw, 'cp', axis_index_groups=CHIPS)  136 us
    reduce_scatter x1, waiting for transfers between devices, local_step(): lax.psum_scatter(dc, 'cp', scatter_dimension=0, tiled=True).astype(BF16)  41.7 us
    pallas_call x1, Pallas kernels, local_step(): pl.pallas_call(attn_kernel, out_shape=(jax.ShapeDtypeStruct((HPC, CH, NOP...  25.7 us
    reduce_scatter x1, waiting for transfers between devices, local_step(): lax.psum_scatter(dr[:, :ROPE], 'cp', scatter_dimension=0, tiled=True)  20.9 us
    all_gather x1, waiting for transfers between devices, local_step(): dw = lax.all_gather(dw, 'cp', axis_index_groups=PAIRS)  17.6 us
    slice x3, local copies, waits for them, and re-layouts, local_step(): return (attn_out, d_query, d_latent, d_key_rope, dw[0], dw[1])  15.1 us
    unnamed x16, local copies, waits for them, and re-layouts  14.5 us
    reshape x1, local copies, waits for them, and re-layouts, local_step(): dw = dw.reshape(2, 4, LAT, 2, 2, NOPE)  10.5 us
  transfers between devices with their start and end apart: 9, of which 6 were waited for; matrix products, arithmetic and copies ran while one was open for 11% of the time, Pallas kernels for 0%

profile of v1, /device:TPU:0, one launch (start us, length us, event | category | flops | bytes accessed | tf_op | source)
XLA Modules:
  0.0 334.0 jit_solution(7640178747168661405)
XLA Ops:
  7.2 0.9 copy.37
  8.1 0.1 pad.13.clone
  8.2 1.7 maximum_maximum_fusion
  10.0 2.7 copy.34
  12.8 1.2 fusion.1
  13.9 0.9 collective-permute-start
  14.8 0.9 constant_dynamic-slice_fusion.5
  15.7 0.9 copy.57
  16.5 0.3 collective-permute-start.1
  16.9 2.6 constant_dynamic-slice_fusion.2
  19.5 2.4 copy.50
  21.9 2.3 copy.41
  24.2 1.4 copy.49
  25.6 2.3 copy.39
  28.0 2.8 pad_maximum_fusion.1.w_ref
  30.8 1.1 broadcast_select_fusion.7
  31.9 1.0 pad_maximum_fusion.2.do_ref
  33.0 1.7 broadcast_select_fusion.3
  34.7 1.5 pad_maximum_fusion.q_ref
  36.1 0.9 all-gather.3.cloned.1.call-done
  37.1 1.9 slice.27.r_ref
  39.0 3.1 slice.26.c_ref
  42.1 25.7 %shard_map.109 = (bf16[8,512,128]{2,1,0:T(8,128)(2,1)}, bf16[8,512,256]{2,1,0:T(8,128)(2,1)}, f32[4,512,512]{2,1,0:T(8,128)}, f32[2048,512]{1,0:T(8,128)}, f32[2048,128]{1,0:T(8,128)}) custom-call(bf16[8,512,256]{2,1,0:T(8,128)(2,1)} %pad_maximum_fusion.q_ref, bf16[8,512,128]{2,1,0:T(8,128)(2,1)} %pad_maximum_fusion.2.do_ref, ...), custom_call_target="tpu_custom_call" | custom-call | flops 30000001024 | bytes 20971520 | tf_op jit(solution)/shard_map/pallas_call | solution.py:172
  67.9 0.7 reduce-scatter.5.cloned.1.call-update
  68.6 0.5 reduce-scatter.3.cloned.1.call-update
  69.1 0.2 all-gather.5.cloned.1.call-start
  69.4 136.2 %all-reduce.3.cloned.1.call-done = f32[1,4,512,512]{3,2,1,0:T(8,128)} async-done(((f32[1,4,512,512]{3,2,1,0:T(8,128)}), f32[1,4,512,512]{3,2,1,0:T(8,128)}) %all-reduce.3.cloned.1.call-update) | async-done | bytes 4194320 | tf_op jit(solution)/shard_map/psum | solution.py:196
  205.6 1.6 copy-done.1
  207.1 1.0 constant_dynamic-slice_fusion
  208.2 1.9 constant_dynamic-slice_fusion.1
  210.0 0.5 collective-permute-start.2
  210.5 1.5 collective-permute-done.2
  212.1 1.4 broadcast_select_fusion.5
  213.5 0.1 maximum_bitcast_fusion.1
  213.6 1.6 copy.44
  215.3 20.9 %reduce-scatter.5.cloned.1.call-done = f32[256,64]{1,0:T(8,128)} async-done(((f32[2048,64]{1,0:T(8,128)}), f32[256,64]{1,0:T(8,128)}) %reduce-scatter.5.cloned.1.call-update) | async-done | bytes 65552 | tf_op jit(solution)/shard_map/reduce_scatter | solution.py:194
  236.2 0.9 convert_element_type.9
  237.1 0.7 copy.46
  237.8 0.4 broadcast_select_fusion.1
  238.3 0.2 maximum_bitcast_fusion
  238.5 2.3 copy.45
  240.7 41.7 %reduce-scatter.3.cloned.1.call-done = f32[256,512]{1,0:T(8,128)} async-done(((f32[2048,512]{1,0:T(8,128)}), f32[256,512]{1,0:T(8,128)}) %reduce-scatter.3.cloned.1.call-update) | async-done | bytes 524304 | tf_op jit(solution)/shard_map/reduce_scatter | solution.py:193
  282.4 1.8 convert_element_type.8
  284.2 17.6 %all-gather.5.cloned.1.call-done = f32[2,4,512,512]{3,2,1,0:T(8,128)} async-done(((f32[1,4,512,512]{3,2,1,0:T(8,128)}), f32[2,4,512,512]{3,2,1,0:T(8,128)}) %all-gather.5.cloned.1.call-update) | async-done | bytes 8388624 | tf_op jit(solution)/shard_map/all_gather | solution.py:197
  301.8 10.5 %reshape.28 = f32[2,4,512,2,2,128]{5,4,3,2,1,0:T(2,128)} reshape(f32[2,4,512,512]{3,2,1,0:T(8,128)} %all-gather.5.cloned.1.call-done) | data formatting | bytes 16777216 | tf_op jit(solution)/shard_map/reshape | solution.py:198
  312.3 6.0 %fusion.2 = (f32[1,512,2,4,2,128]{5,4,0,1,3,2:T(2,128)}, f32[1,512,2,4,2,128]{5,4,0,1,3,2:T(2,128)S(1)}) fusion(f32[2,512,2,4,2,128]{5,4,0,1,3,2:T(2,128)} %bitcast.33), kind=kLoop, calls=%fused_computation.26 | loop fusion | bytes 16777216 | tf_op jit(solution)/shard_map/slice | solution.py:200
  318.4 5.6 %copy.43 = f32[1,512,2,4,2,128]{5,4,3,2,1,0:T(2,128)} copy(f32[1,512,2,4,2,128]{5,4,0,1,3,2:T(2,128)} %get-tuple-element.34) | data formatting | bytes 8388608 | tf_op jit(solution)/shard_map/slice | solution.py:200
  324.0 3.5 %copy.42 = f32[1,512,2,4,2,128]{5,4,3,2,1,0:T(2,128)} copy(f32[1,512,2,4,2,128]{5,4,0,1,3,2:T(2,128)S(1)} %get-tuple-element.35) | data formatting | bytes 8388608 | tf_op jit(solution)/shard_map/slice | solution.py:200
  (19 shorter events, 0.2 us)
Async XLA Ops:
  7.2 29.9 %all-gather.3.cloned.1.call-start = ((), (), s32[]{:S(2)}) async-start(), calls=%async_computation.2 | async-start | bytes 2949120 | tf_op jit(solution)/shard_map/all_gather | solution.py:163
  9.9 195.6 %all-reduce.3.cloned.1.call-start = ((), (), s32[]{:S(2)}) async-start(), calls=%async_computation.5 | async-start | bytes 8388608 | tf_op jit(solution)/shard_map/psum | solution.py:196
  12.8 2.0 copy-start.3
  13.9 19.1 %collective-permute-start = (bf16[8,256,256]{2,1,0:T(8,128)(2,1)}, bf16[8,256,256]{2,1,0:T(8,128)(2,1)}, u32[]{:S(2)}, u32[]{:S(2)}) collective-permute-start(bf16[8,256,256]{2,1,0:T(8,128)(2,1)} %fusion.1), channel_id=1, source_target_pairs={{0,1},{1,0},{2,3},{3,2},{4,5},{5,4},{6,7},{7,6}} | collective-permute-start | bytes 3145736 | tf_op jit(solution)/shard_map/ppermute | solution.py:147
  16.5 14.2 %collective-permute-start.1 = (bf16[8,256,128]{2,1,0:T(8,128)(2,1)}, bf16[8,256,128]{2,1,0:T(8,128)(2,1)}, u32[]{:S(2)}, u32[]{:S(2)}) collective-permute-start(bf16[8,256,128]{2,1,0:T(8,128)(2,1)} %bitcast.30), channel_id=1, source_target_pairs={{0,1},{1,0},{2,3},{3,2},{4,5},{5,4},{6,7},{7,6}} | collective-permute-start | bytes 1572872 | tf_op jit(solution)/shard_map/ppermute | solution.py:147
  25.6 2.4 copy-start
  28.0 2.8 copy-start.2
  67.8 168.4 %reduce-scatter.5.cloned.1.call-start = ((), (), s32[]{:S(2)}) async-start(), calls=%async_computation.4 | async-start | bytes 1179648 | tf_op jit(solution)/shard_map/reduce_scatter | solution.py:194
  68.6 213.9 %reduce-scatter.3.cloned.1.call-start = ((), (), s32[]{:S(2)}) async-start(), calls=%async_computation.3 | async-start | bytes 4718592 | tf_op jit(solution)/shard_map/reduce_scatter | solution.py:193
  69.1 232.7 %all-gather.5.cloned.1.call-start = ((), (), s32[]{:S(2)}) async-start(), calls=%async_computation.6 | async-start | bytes 12582912 | tf_op jit(solution)/shard_map/all_gather | solution.py:197
  205.5 1.6 copy-start.1
  208.2 29.7 %collective-permute-start.3 = (bf16[8,256,256]{2,1,0:T(8,128)(2,1)}, bf16[8,256,256]{2,1,0:T(8,128)(2,1)S(1)}, u32[]{:S(2)}, u32[]{:S(2)}) collective-permute-start(bf16[8,256,256]{2,1,0:T(8,128)(2,1)} %constant_dynamic-slice_fusion), channel_id=1, source_target_pairs={{0,1},{1,0},{2,3},{3,2},{4,5},{5,4},{6,7},{7,6}} | collective-permute-start | bytes 3145736 | tf_op jit(solution)/shard_map/ppermute | solution.py:155
  210.0 2.0 collective-permute-start.2
Sparse Core Ops, SparseCore 0:
  10.1 26.9 all-gather.2
  67.9 137.5 all-reduce.2
  208.6 27.5 reduce-scatter.4
  239.9 42.4 reduce-scatter.2
  283.8 18.0 all-gather.4

commit v2 on v1

v2 whole, which is shorter than its diff:
```python
import math
import jax
import jax.numpy as jnp
from jax import lax
from jax.experimental import pallas as pl
from jax.experimental.pallas import tpu as pltpu
from jax.sharding import PartitionSpec as P

F32 = jnp.float32
BF16 = jnp.bfloat16
TOK = 256
CH = 512
HPC = 8
NS = HPC // 2
NOPE = 128
ROPE = 64
LAT = 512
CRW = LAT + NOPE
NCHIP = 4
SEQ = CH * NCHIP
MESH = pl.DeviceIdType.MESH
A_COLS = pl.ds(0, 256)
B_COLS = pl.ds(256, 256)


def nt(a, b):
    return lax.dot_general(a, b, (((1,), (1,)), ((), ())), preferred_element_type=F32)


def nn(a, b):
    return lax.dot_general(a, b, (((1,), (0,)), ((), ())), preferred_element_type=F32)


def tn(a, b):
    return lax.dot_general(a, b, (((0,), (0,)), ((), ())), preferred_element_type=F32)


def mul(i, n):
    return pl.multiple_of(i * n, n)


def attn_kernel(q_in, do_in, cr_in, wk_in, wv_in,
                o_out, dq_out, dw_out, dlat_out, dr_out,
                q_ref, do_ref, cr_ref, wk, wv, o_ref, dq_ref, dw_ref, dwo, dcr,
                ct, kv, qt, dot_, s_buf, p_buf, rb1, rb2, rbd, rbe,
                lsem, xs, xr, cs, crs, ws, wr, fs, fr, fl, ds_, dr_s):
    scale = 1.0 / math.sqrt(NOPE + ROPE)
    c2 = scale * math.log2(math.e)
    me = lax.axis_index("cp")
    core = lax.rem(me, 2)
    chip = lax.div(me, 2)
    x = lax.rem(chip, 2)
    y = lax.div(chip, 2)
    partner = me + 1 - 2 * core
    xn = me + 2 - 4 * x
    yn = me + 4 - 8 * y
    dn = xn + 4 - 8 * y
    chip_x = chip + 1 - 2 * x
    chip_y = chip + 2 - 4 * y
    chip_d = chip_x + 2 - 4 * y

    def rcopy(src, dst, ss, rs, dev):
        return pltpu.make_async_remote_copy(src_ref=src, dst_ref=dst, send_sem=ss, recv_sem=rs,
                                            device_id=(dev,), device_id_type=MESH)

    bar = pltpu.get_barrier_semaphore()
    for peer in (partner, xn, yn, dn):
        pl.semaphore_signal(bar, inc=1, device_id=(peer,), device_id_type=MESH)
    pl.semaphore_wait(bar, 4)

    my_rows = pl.ds(mul(me, TOK), TOK)
    own_rows = pl.ds(mul(core, TOK), TOK)
    oth_rows = pl.ds(mul(1 - core, TOK), TOK)
    mine = pl.ds(mul(core, HPC), HPC)
    other = pl.ds(mul(1 - core, HPC), HPC)
    c_direct = [rcopy(cr_in, cr_ref.at[my_rows], cs.at[i], crs.at[i], dev)
                for i, dev in enumerate((partner, dn, xn, yn))]
    for cp in c_direct:
        cp.start()
    local = [pltpu.make_async_copy(cr_in, cr_ref.at[my_rows], lsem.at[0]),
             pltpu.make_async_copy(q_in.at[mine], q_ref.at[:, own_rows], lsem.at[1]),
             pltpu.make_async_copy(do_in.at[mine], do_ref.at[:, own_rows], lsem.at[2]),
             pltpu.make_async_copy(wk_in, wk, lsem.at[3]),
             pltpu.make_async_copy(wv_in, wv, lsem.at[4])]
    heads = [rcopy(q_in.at[other], q_ref.at[:, own_rows], xs.at[0], xr.at[0], partner),
             rcopy(do_in.at[other], do_ref.at[:, own_rows], xs.at[1], xr.at[1], partner)]
    for cp in heads + local:
        cp.start()
    dcr[...] = jnp.zeros_like(dcr)
    for cp in heads + local:
        cp.wait()
    c_direct[0].wait()

    c_fwd = []
    for i, src in ((1, dn), (2, xn), (3, yn)):
        rows = pl.ds(mul(src, TOK), TOK)
        c_fwd.append(rcopy(cr_ref.at[rows], cr_ref.at[rows], cs.at[3 + i], crs.at[3 + i], partner))

    def wait_latents():
        for i in (2, 3, 1):
            c_direct[i].wait()
            c_fwd[i - 1].start()
        for cp in c_fwd:
            cp.wait()

        def tr_chunk(j, _):
            ct[j] = cr_ref[pl.ds(mul(j, CH), CH), :LAT].T
            return 0
        lax.fori_loop(0, chip + 1, tr_chunk, 0)

    hx = pl.ds(mul(x, 256), 256)
    hx1 = pl.ds(mul(1 - x, 256), 256)
    hy = pl.ds(mul(y, 256), 256)
    hy1 = pl.ds(mul(1 - y, 256), 256)
    qa = pl.ds(pl.multiple_of(x * 256 + y * 128, 128), 128)
    qa1 = pl.ds(pl.multiple_of(x * 256 + (1 - y) * 128, 128), 128)
    qb = pl.ds(pl.multiple_of(y * 256 + x * 128, 128), 128)
    qb1 = pl.ds(pl.multiple_of(y * 256 + (1 - x) * 128, 128), 128)

    def w_copy(phase, s):
        if phase == 1:
            pair = ((dw_ref.at[s, hx1, A_COLS], rb1.at[0], xn), (dw_ref.at[s, hy1, B_COLS], rb1.at[1], yn))
        elif phase == 2:
            pair = ((dw_ref.at[s, qa1, A_COLS], rb2.at[0], yn), (dw_ref.at[s, qb1, B_COLS], rb2.at[1], xn))
        elif phase == 3:
            pair = ((dwo.at[s, qa, A_COLS], dwo.at[s, qa, A_COLS], yn),
                    (dwo.at[s, qb, B_COLS], dwo.at[s, qb, B_COLS], xn))
        else:
            pair = ((dwo.at[s, hx, A_COLS], dwo.at[s, hx, A_COLS], xn),
                    (dwo.at[s, hy, B_COLS], dwo.at[s, hy, B_COLS], yn))
        return [rcopy(a, b, ws.at[phase - 1, i], wr.at[phase - 1, i], d) for i, (a, b, d) in enumerate(pair)]

    def w_start(phase, s):
        for cp in w_copy(phase, s):
            cp.start()

    def w_wait(phase, s):
        for cp in w_copy(phase, s):
            cp.wait()

    def finish1(s):
        w_wait(1, s)
        dw_ref[s, hx, A_COLS] += rb1[0]
        dw_ref[s, hy, B_COLS] += rb1[1]
        w_start(2, s)

    def finish2(s):
        w_wait(2, s)
        dwo[s, qa, A_COLS] = dw_ref[s, qa, A_COLS] + rb2[0]
        dwo[s, qb, B_COLS] = dw_ref[s, qb, B_COLS] + rb2[1]
        w_start(3, s)

    def finish3(s):
        w_wait(3, s)
        w_start(4, s)

    def w_final(s):
        slot = core * NS + s
        return (pltpu.make_async_copy(dwo.at[s], dw_out.at[slot], fl.at[s]),
                rcopy(dwo.at[s], dw_out.at[slot], fs.at[s], fr.at[s], partner))

    def finish4(s):
        w_wait(4, s)
        for cp in w_final(s):
            cp.start()

    def step(s, _):
        dw_ref[s] = jnp.zeros((LAT, 4 * NOPE), F32)
        for a in range(2):
            h = 2 * s + a
            qt[a] = q_ref[h].T
            dot_[a] = do_ref[h].T
        w_s = jnp.concatenate([wk[2 * s], wk[2 * s + 1], wv[2 * s], wv[2 * s + 1]], axis=1)

        def phase1(j, stats, masked):
            rows = pl.ds(mul(j, CH), CH)
            kvv = nn(cr_ref[rows, :LAT], w_s).astype(BF16)
            kv[rows, :] = kvv
            rp = cr_ref[rows, LAT:]
            out = []
            for a in range(2):
                k_cat = jnp.concatenate([kvv[:, a * NOPE:(a + 1) * NOPE], rp], axis=1)
                s2 = nn(k_cat, qt[a]) * c2
                if masked:
                    ki = lax.broadcasted_iota(jnp.int32, (CH, CH), 0)
                    qi = lax.broadcasted_iota(jnp.int32, (CH, CH), 1)
                    s2 = jnp.where(ki <= qi, s2, -1e30)
                s_buf[a, rows, :] = s2
                cm = jnp.max(s2, axis=0, keepdims=True)
                if stats is None:
                    m = cm
                    l = jnp.sum(jnp.exp2(s2 - m), axis=0, keepdims=True)
                else:
                    m0, l0 = stats[a]
                    m = jnp.maximum(m0, cm)
                    l = l0 * jnp.exp2(m0 - m) + jnp.sum(jnp.exp2(s2 - m), axis=0, keepdims=True)
                out.append((m, l))
            return tuple(out)

        stats = phase1(chip, None, True)

        @pl.when(s == 0)
        def _():
            wait_latents()

        stats = lax.fori_loop(0, chip, lambda j, st: phase1(j, st, False), stats)
        lse = [m + jnp.log2(l) for m, l in stats]

        @pl.when(s > 1)
        def _():
            finish4(s - 2)

        @pl.when(s > 0)
        def _():
            finish1(s - 1)

        def phase2(j, acc):
            rows = pl.ds(mul(j, CH), CH)
            out = []
            for a in range(2):
                pb = jnp.exp2(s_buf[a, rows, :] - lse[a]).astype(BF16)
                p_buf[a, rows, :] = pb
                v = kv[rows, (2 + a) * NOPE:(3 + a) * NOPE]
                out.append(acc[a] + tn(v, pb))
            return tuple(out)

        ot = lax.fori_loop(0, chip + 1, phase2, tuple(jnp.zeros((NOPE, CH), F32) for _ in range(2)))
        delta = []
        for a in range(2):
            h = 2 * s + a
            delta.append(jnp.sum(ot[a] * dot_[a].astype(F32), axis=0, keepdims=True))
            o_ref[h] = ot[a].T.astype(BF16)

        @pl.when(s > 0)
        def _():
            finish2(s - 1)

        def phase3(j, acc):
            rows = pl.ds(mul(j, CH), CH)
            dks, dvs, out = [], [], []
            rp = cr_ref[rows, LAT:]
            dr = jnp.zeros((CH, NOPE), F32)
            for a in range(2):
                h = 2 * s + a
                k = kv[rows, a * NOPE:(a + 1) * NOPE]
                v = kv[rows, (2 + a) * NOPE:(3 + a) * NOPE]
                pb = p_buf[a, rows, :]
                dp = nn(v, dot_[a])
                ds = (pb.astype(F32) * (dp - delta[a])).astype(BF16)
                k_cat = jnp.concatenate([k, rp], axis=1)
                out.append(acc[a] + tn(k_cat, ds))
                dkr = nn(ds, q_ref[h]) * scale
                dks.append(dkr[:, :NOPE].astype(BF16))
                dr = dr + dkr[:, NOPE:]
                dvs.append(nn(pb, do_ref[h]).astype(BF16))
            dkv = jnp.concatenate(dks + dvs, axis=1)
            dcr[j, :, LAT:] += dr
            dcr[j, :, :LAT] += nt(dkv, w_s)
            dw_ref[s] += nn(ct[j], dkv)
            return tuple(out)

        dqt = lax.fori_loop(0, chip + 1, phase3, tuple(jnp.zeros((2 * NOPE, CH), F32) for _ in range(2)))
        for a in range(2):
            dq_ref[2 * s + a] = (dqt[a].T * scale).astype(BF16)

        @pl.when(s > 0)
        def _():
            finish3(s - 1)

        w_start(1, s)
        return 0

    lax.fori_loop(0, NS, step, 0)

    d1 = rcopy(dcr.at[:, oth_rows], rbd, ds_.at[0], dr_s.at[0], partner)
    d1.start()
    outs = [pltpu.make_async_copy(o_ref.at[:, own_rows], o_out.at[mine], lsem.at[5]),
            pltpu.make_async_copy(dq_ref.at[:, own_rows], dq_out.at[mine], lsem.at[6]),
            rcopy(o_ref.at[:, oth_rows], o_out.at[mine], xs.at[2], xr.at[2], partner),
            rcopy(dq_ref.at[:, oth_rows], dq_out.at[mine], xs.at[3], xr.at[3], partner)]
    for cp in outs:
        cp.start()
    d1.wait()
    dcr[:, own_rows, :] += rbd[...]

    kinds = ((chip_d, dn), (chip_x, xn), (chip_y, yn))
    d2 = [rcopy(dcr.at[ch, own_rows], rbe.at[i], ds_.at[1 + i], dr_s.at[1 + i], dev)
          for i, (ch, dev) in enumerate(kinds)]
    finish4(NS - 2)
    finish1(NS - 1)
    for i, (ch, dev) in enumerate(kinds):
        @pl.when(ch < chip)
        def _(i=i):
            d2[i].start()
    finish2(NS - 1)
    finish3(NS - 1)
    for i, (ch, dev) in enumerate(kinds):
        @pl.when(ch > chip)
        def _(i=i):
            d2[i].wait_recv()
            dcr[chip, own_rows, :] += rbe[i]

        @pl.when(ch < chip)
        def _(i=i):
            d2[i].wait_send()
    dlat_out[...] = dcr[chip, own_rows, :LAT].astype(BF16)
    dr_out[...] = dcr[chip, own_rows, LAT:LAT + ROPE].astype(BF16)
    finish4(NS - 1)
    for cp in outs:
        cp.wait()
    for s in range(NS):
        for cp in w_final(s):
            cp.wait()


def solution(mesh):
    seq_spec = P("cp")

    def local_step(queries, latent, key_rope, w_uk, w_uv, d_out):
        core = lax.rem(lax.axis_index("cp"), 2)

        q_t = jnp.transpose(jnp.pad(queries, ((0, 0), (0, 0), (0, 64))), (1, 0, 2))
        do_t = jnp.transpose(d_out, (1, 0, 2))
        cr = jnp.concatenate([latent, key_rope, jnp.zeros((TOK, 64), BF16)], axis=1)

        def w_half(w):
            return jnp.transpose(lax.dynamic_slice_in_dim(w, core * HPC, HPC, axis=1), (1, 0, 2))

        any_spec = pl.BlockSpec(memory_space=pl.ANY)
        vm_spec = pl.BlockSpec(memory_space=pltpu.VMEM)
        dma = pltpu.SemaphoreType.DMA
        o_t, dq_t, dw, d_latent, d_key_rope = pl.pallas_call(
            attn_kernel,
            out_shape=(jax.ShapeDtypeStruct((2 * HPC, TOK, NOPE), BF16),
                       jax.ShapeDtypeStruct((2 * HPC, TOK, 2 * NOPE), BF16),
                       jax.ShapeDtypeStruct((2 * NS, LAT, 4 * NOPE), F32),
                       jax.ShapeDtypeStruct((TOK, LAT), BF16),
                       jax.ShapeDtypeStruct((TOK, ROPE), BF16)),
            in_specs=[any_spec] * 5,
            out_specs=[any_spec] * 3 + [vm_spec] * 2,
            scratch_shapes=[pltpu.VMEM((HPC, CH, 2 * NOPE), BF16),
                            pltpu.VMEM((HPC, CH, NOPE), BF16),
                            pltpu.VMEM((SEQ, CRW), BF16),
                            pltpu.VMEM((HPC, LAT, NOPE), BF16),
                            pltpu.VMEM((HPC, LAT, NOPE), BF16),
                            pltpu.VMEM((HPC, CH, NOPE), BF16),
                            pltpu.VMEM((HPC, CH, 2 * NOPE), BF16),
                            pltpu.VMEM((NS, LAT, 4 * NOPE), F32),
                            pltpu.VMEM((NS, LAT, 4 * NOPE), F32),
                            pltpu.VMEM((NCHIP, CH, CRW), F32),
                            pltpu.VMEM((NCHIP, LAT, CH), BF16),
                            pltpu.VMEM((SEQ, 4 * NOPE), BF16),
                            pltpu.VMEM((2, 2 * NOPE, CH), BF16),
                            pltpu.VMEM((2, NOPE, CH), BF16),
                            pltpu.VMEM((2, SEQ, CH), F32),
                            pltpu.VMEM((2, SEQ, CH), BF16),
                            pltpu.VMEM((2, 256, 256), F32),
                            pltpu.VMEM((2, 128, 256), F32),
                            pltpu.VMEM((NCHIP, TOK, CRW), F32),
                            pltpu.VMEM((3, TOK, CRW), F32),
                            dma((7,)), dma((4,)), dma((4,)), dma((7,)), dma((7,)),
                            dma((4, 2)), dma((4, 2)), dma((NS,)), dma((NS,)), dma((NS,)),
                            dma((4,)), dma((4,))],
            compiler_params=pltpu.CompilerParams(vmem_limit_bytes=62 << 20, collective_id=0, has_side_effects=True),
            cost_estimate=pl.CostEstimate(flops=30 * 10**9, bytes_accessed=20 << 20, transcendentals=10**7),
        )(q_t, do_t, cr, w_half(w_uk), w_half(w_uv))

        attn_out = jnp.transpose(o_t, (1, 0, 2))
        d_query = jnp.transpose(dq_t, (1, 0, 2))[:, :, :NOPE + ROPE]
        dw = dw.reshape(2 * NS, LAT, 2, 2, NOPE)
        dw = jnp.transpose(dw, (2, 1, 0, 3, 4)).reshape(2, LAT, 16, NOPE)
        return attn_out, d_query, d_latent, d_key_rope, dw[0], dw[1]

    return jax.shard_map(local_step, mesh=mesh,
                         in_specs=(seq_spec, seq_spec, seq_spec, P(), P(), seq_spec),
                         out_specs=(seq_spec, seq_spec, seq_spec, seq_spec, P(), P()),
                         check_vma=False)
```

time: 335 us -> 208 us (0.62)
  waiting for transfers between devices: 220 us -> 0 us
  Pallas kernels: 25.7 us -> 161 us
  local copies, waits for them, and re-layouts: 57.4 us -> 44 us
  between operations: 13.9 us -> 0.7 us
  other arithmetic: 14.7 us -> 1.75 us
    psum x1 -> x0, waiting for transfers between devices: 136 us -> none  [local_step(): dw = lax.psum(dw, 'cp', axis_index_groups=CHIPS)]
    pallas_call x1, Pallas kernels: 25.7 us -> 161 us  [local_step(): pl.pallas_call(attn_kernel, out_shape=(jax.ShapeDtypeStruct((2 * HPC, TOK...]
    reduce_scatter x2 -> x0, waiting for transfers between devices: 62.6 us -> none  [the longest x1 41.7 us: local_step(): lax.psum_scatter(dc, 'cp', scatter_dimension=0, tiled=True).astype(BF16)]
    all_gather x2 -> x0, waiting for transfers between devices: 18.6 us -> none  [the longest x1 17.6 us: local_step(): dw = lax.all_gather(dw, 'cp', axis_index_groups=PAIRS)]
    dynamic_slice x4 -> x1, local copies, waits for them, and re-layouts: 6.71 us -> 1.36 us  [w_half(): lax.dynamic_slice_in_dim(w, core * HPC, HPC, axis=1)]
    concatenate x3 -> x0, other arithmetic: 5.35 us -> none  [the longest x1 2.81 us: local_step(): wcat = jnp.concatenate([w_half(w_uk), w_half(w_uv)], axis=2)]
    slice x2 -> x0, local copies, waits for them, and re-layouts: 4.99 us -> none  [local_step(): c_all, r_all = (cr_all[:, :LAT], cr_all[:, LAT:])]
    select_n x4 -> x0, other arithmetic: 4.69 us -> none  [the longest x2 2.81 us: heads_of_core(): first = jnp.where(core == 0, mine, got)]
  transfers between devices with their start and end apart: 9 -> 0, of which waited for: 6 -> 0; matrix products, arithmetic and copies ran while one was open for 11% -> 0% of each run, Pallas kernels for 0% -> 0%
where the time goes in v2:
time: 208 us
  Pallas kernels  161 us (77%)
  local copies, waits for them, and re-layouts  44 us (21%)
    pallas_call x1, Pallas kernels, local_step(): pl.pallas_call(attn_kernel, out_shape=(jax.ShapeDtypeStruct((2 * HPC, TOK...  161 us
    unnamed x17, local copies, waits for them, and re-layouts  15.2 us
    slice x3, local copies, waits for them, and re-layouts, local_step(): return (attn_out, d_query, d_latent, d_key_rope, dw[0], dw[1])  15.1 us
    reshape x1, local copies, waits for them, and re-layouts, local_step(): dw = dw.reshape(2 * NS, LAT, 2, 2, NOPE)  10.5 us

profile of v2, /device:TPU:0, one launch (start us, length us, event | category | flops | bytes accessed | tf_op | source)
XLA Modules:
  0.0 207.9 jit_solution(18150362918334617231)
XLA Ops:
  0.6 0.0 copy-start.1
  0.7 0.1 pad.7.clone
  0.7 1.0 copy.14
  1.7 1.7 maximum_maximum_fusion.cr_in
  3.5 2.5 %copy.29 = bf16[256,16,128]{2,0,1:T(8,128)(2,1)} copy(bf16[256,16,128]{2,1,0:T(8,128)(2,1)} %param.11) | data formatting | bytes 2097152 | tf_op args[5]
  6.0 0.0 copy-done.1
  6.0 1.4 constant_dynamic-slice_fusion
  7.3 1.1 copy.27
  8.5 1.1 copy.28
  9.6 2.7 %copy.12 = bf16[256,16,192]{2,0,1:T(8,128)(2,1)S(1)} copy(bf16[256,16,192]{0,2,1:T(8,128)(2,1)} %param.6) | data formatting | bytes 3145728 | tf_op args[0]
  12.3 1.7 pad_bitcast_fusion.q_in
  14.1 161.5 %shard_map.109 = (bf16[16,256,128]{2,1,0:T(8,128)(2,1)}, bf16[16,256,256]{2,1,0:T(8,128)(2,1)}, f32[8,512,512]{2,1,0:T(8,128)}, bf16[256,512]{1,0:T(8,128)(2,1)}, bf16[256,64]{1,0:T(8,128)(2,1)}) custom-call(bf16[16,256,256]{2,1,0:T(8,128)(2,1)} %pad_bitcast_fusion.q_in, bf16[16,256,128]{2,1,0:T(8,128)(2,1)} %bitcast.21, ...), custom_call_target="tpu_custom_call" | custom-call | flops 30000001024 | bytes 20971520 | tf_op jit(solution)/shard_map/pallas_call | solution.py:332
  175.6 0.0 copy-start
  175.6 3.0 %copy.19 = bf16[256,16,128]{2,1,0:T(8,128)(2,1)} copy(bf16[256,16,128]{2,0,1:T(8,128)(2,1)} %bitcast.24) | data formatting | bytes 2097152
  178.6 0.0 copy-start.3
  178.6 0.0 copy-done
  178.6 2.2 %copy.20 = bf16[256,16,192]{0,2,1:T(8,128)(2,1)} copy(bf16[256,16,192]{2,0,1:T(8,128)(2,1)S(1)} %bitcast.20) | data formatting | bytes 3145728
  180.8 0.0 copy-done.3
  180.8 0.7 copy.21
  181.6 10.5 %reshape.20 = f32[8,512,2,2,128]{4,3,2,1,0:T(2,128)} reshape(f32[8,512,512]{2,1,0:T(8,128)} %get-tuple-element.15) | data formatting | bytes 16777216 | tf_op jit(solution)/shard_map/reshape | solution.py:370
  192.1 6.0 %fusion = (f32[1,512,8,2,128]{4,3,0,1,2:T(2,128)}, f32[1,512,8,2,128]{4,3,0,1,2:T(2,128)S(1)}) fusion(f32[2,512,8,2,128]{4,3,0,1,2:T(2,128)} %bitcast.17), kind=kLoop, calls=%fused_computation.7 | loop fusion | bytes 16777216 | tf_op jit(solution)/shard_map/slice | solution.py:372
  198.1 5.6 %copy.18 = f32[1,512,8,2,128]{4,3,2,1,0:T(2,128)} copy(f32[1,512,8,2,128]{4,3,0,1,2:T(2,128)} %get-tuple-element.22) | data formatting | bytes 8388608 | tf_op jit(solution)/shard_map/slice | solution.py:372
  203.7 0.0 copy-start.2
  203.7 3.5 %copy.17 = f32[1,512,8,2,128]{4,3,2,1,0:T(2,128)} copy(f32[1,512,8,2,128]{4,3,0,1,2:T(2,128)S(1)} %get-tuple-element.23) | data formatting | bytes 8388608 | tf_op jit(solution)/shard_map/slice | solution.py:372
  207.2 0.0 copy-done.2
  207.2 0.7 copy.31
  (1 shorter events, 0.0 us)
Async XLA Ops:
  0.6 5.3 %copy-start.1 = (bf16[512,16,128]{2,1,0:T(8,128)(2,1)S(1)}, bf16[512,16,128]{2,1,0:T(8,128)(2,1)}, u32[]{:S(2)}) copy-start(bf16[512,16,128]{2,1,0:T(8,128)(2,1)} %param.10) | copy-start | bytes 6291460
  175.6 3.0 %copy-start = (bf16[16,256,256]{2,1,0:T(8,128)(2,1)S(1)}, bf16[16,256,256]{2,1,0:T(8,128)(2,1)}, u32[]{:S(2)}) copy-start(bf16[16,256,256]{2,1,0:T(8,128)(2,1)} %get-tuple-element.12) | copy-start | bytes 6291460
  178.6 2.3 %copy-start.3 = (bf16[256,64]{1,0:T(8,128)(2,1)S(1)}, bf16[256,64]{1,0:T(8,128)(2,1)}, u32[]{:S(2)}) copy-start(bf16[256,64]{1,0:T(8,128)(2,1)} %get-tuple-element.19) | copy-start | bytes 98308
  203.7 3.5 %copy-start.2 = (bf16[256,512]{1,0:T(8,128)(2,1)S(1)}, bf16[256,512]{1,0:T(8,128)(2,1)}, u32[]{:S(2)}) copy-start(bf16[256,512]{1,0:T(8,128)(2,1)} %get-tuple-element.34) | copy-start | bytes 786436

commit v3 on v2

v3 whole, which is shorter than its diff:
```python
import math
import jax
import jax.numpy as jnp
from jax import lax
from jax.experimental import pallas as pl
from jax.experimental.pallas import tpu as pltpu
from jax.sharding import PartitionSpec as P

F32 = jnp.float32
BF16 = jnp.bfloat16
TOK = 256
CH = 512
HEADS = 16
HPC = 8
G = 2
NS = HPC // G
NOPE = 128
ROPE = 64
QK = NOPE + ROPE
LAT = 512
GW = G * NOPE
MSG = TOK + ROPE // 2
NCHIP = 4
SEQ = CH * NCHIP
MESH = pl.DeviceIdType.MESH
A_COLS = pl.ds(0, GW)
B_COLS = pl.ds(GW, GW)


def nt(a, b):
    return lax.dot_general(a, b, (((1,), (1,)), ((), ())), preferred_element_type=F32)


def nn(a, b):
    return lax.dot_general(a, b, (((1,), (0,)), ((), ())), preferred_element_type=F32)


def tn(a, b):
    return lax.dot_general(a, b, (((0,), (0,)), ((), ())), preferred_element_type=F32)


def mul(i, n):
    return pl.multiple_of(i * n, n)


def attn_kernel(q_in, do_in, c_in, r_in, wk_in, wv_in,
                o_out, dq_out, dw_out, dlat_out, dr_out,
                do_raw, wk_raw, wv_raw, stage, do_snd,
                qt, do_ref, c_ref, rt, rn, wk, wv, o_ref, dq_ref, dw_ref, dwo, dcr, drr, msg,
                ct, kv, qn, dot_, s_buf, p_buf, rb1, rb2, rbd, rbr, rbe, rly,
                lsem, xs, xr, cs, crs, ws, wr, fs, fr, fl, d1s, d1r, d2s, d2r):
    scale = 1.0 / math.sqrt(QK)
    c2 = scale * math.log2(math.e)
    me = lax.axis_index("cp")
    core = lax.rem(me, 2)
    chip = lax.div(me, 2)
    x = lax.rem(chip, 2)
    y = lax.div(chip, 2)
    partner = me + 1 - 2 * core
    xn = me + 2 - 4 * x
    yn = me + 4 - 8 * y
    dn = xn + 4 - 8 * y
    chip_x = chip + 1 - 2 * x
    chip_y = chip + 2 - 4 * y
    chip_d = chip_x + 2 - 4 * y

    def rcopy(src, dst, ss, rs, dev):
        return pltpu.make_async_remote_copy(src_ref=src, dst_ref=dst, send_sem=ss, recv_sem=rs,
                                            device_id=(dev,), device_id_type=MESH)

    my_rows = pl.ds(mul(me, TOK), TOK)
    own_rows = pl.ds(mul(core, TOK), TOK)
    oth_rows = pl.ds(mul(1 - core, TOK), TOK)
    mine = pl.ds(mul(core, HPC), HPC)

    other = pl.ds(mul(1 - core, HPC), HPC)

    local = [pltpu.make_async_copy(c_in, c_ref.at[my_rows], lsem.at[0]),
             pltpu.make_async_copy(r_in, rt.at[:, my_rows], lsem.at[1]),
             pltpu.make_async_copy(q_in.at[mine], qt.at[:, :, own_rows], lsem.at[2]),
             pltpu.make_async_copy(do_in, do_raw, lsem.at[3]),
             pltpu.make_async_copy(wk_in.at[:, mine], wk_raw, lsem.at[4]),
             pltpu.make_async_copy(wv_in.at[:, mine], wv_raw, lsem.at[5])]
    for cp in local:
        cp.start()

    bar = pltpu.get_barrier_semaphore()
    for peer in (partner, xn, yn, dn):
        pl.semaphore_signal(bar, inc=1, device_id=(peer,), device_id_type=MESH)
    pl.semaphore_wait(bar, 4)

    local[0].wait()
    local[1].wait()

    def latent_copies(i, src, dev):
        rows = pl.ds(mul(src, TOK), TOK)
        return (rcopy(c_ref.at[rows], c_ref.at[rows], cs.at[0, i], crs.at[0, i], dev),
                rcopy(rt.at[:, rows], rt.at[:, rows], cs.at[1, i], crs.at[1, i], dev))

    c_direct = [latent_copies(i, me, dev) for i, dev in enumerate((partner, dn, xn, yn))]
    for pair in c_direct:
        for cp in pair:
            cp.start()

    heads = [rcopy(q_in.at[other], qt.at[:, :, own_rows], xs.at[0], xr.at[0], partner),
             rcopy(do_snd, do_ref.at[:, own_rows], xs.at[1], xr.at[1], partner)]
    heads[0].start()
    local[3].wait()

    def pick(h, rows, stride):
        return stage[pl.ds(h, rows, stride=stride), :].astype(BF16)

    def widen(i, _):
        rows = pl.ds(mul(i, 256), 256)
        stage[rows, :] = do_raw[rows, :].astype(F32)
        return 0
    lax.fori_loop(0, TOK * HEADS // 256, widen, 0)
    is0 = core == 0
    for i in range(HPC):
        lo = pick(i, TOK, HEADS)
        hi = pick(i + HPC, TOK, HEADS)
        do_ref[i, own_rows, :] = jnp.where(is0, lo, hi)
        do_snd[i] = jnp.where(is0, hi, lo)
    heads[1].start()
    for t, (raw, out) in enumerate(((wk_raw, wk), (wv_raw, wv))):
        local[4 + t].wait()

        def body(i, _, raw=raw):
            ls = pl.ds(mul(i, 32), 32)
            stage[pl.ds(mul(i, 256), 256), :] = raw[ls].astype(F32).reshape(256, NOPE)
            return 0
        lax.fori_loop(0, LAT // 32, body, 0)
        for i in range(HPC):
            out[i] = pick(i, LAT, HPC)

    def zero_dc(j, _):
        dcr[j] = jnp.zeros((CH, LAT), F32)
        drr[j] = jnp.zeros((CH, ROPE), F32)
        return 0
    lax.fori_loop(0, chip + 1, zero_dc, 0)
    local[2].wait()
    for cp in heads:
        cp.wait()
    for cp in c_direct[0]:
        cp.wait()

    def turn(j, _):
        rows = pl.ds(mul(j, CH), CH)
        ct[j] = c_ref[rows, :].T
        rn[rows, :] = rt[:, rows].T
        return 0
    turn(chip, 0)

    c_fwd = [latent_copies(3 + i, src, partner) for i, src in ((1, dn), (2, xn), (3, yn))]

    def wait_latents():
        for i in (2, 3, 1):
            for cp in c_direct[i]:
                cp.wait()
            for cp in c_fwd[i - 1]:
                cp.start()
        for pair in c_fwd:
            for cp in pair:
                cp.wait()
        lax.fori_loop(0, chip, turn, 0)

    hx = pl.ds(mul(x, 256), 256)
    hx1 = pl.ds(mul(1 - x, 256), 256)
    hy = pl.ds(mul(y, 256), 256)
    hy1 = pl.ds(mul(1 - y, 256), 256)
    qa = pl.ds(pl.multiple_of(x * 256 + y * 128, 128), 128)
    qa1 = pl.ds(pl.multiple_of(x * 256 + (1 - y) * 128, 128), 128)
    qb = pl.ds(pl.multiple_of(y * 256 + x * 128, 128), 128)
    qb1 = pl.ds(pl.multiple_of(y * 256 + (1 - x) * 128, 128), 128)

    def w_copy(phase, s):
        if phase == 1:
            pair = ((dw_ref.at[s, hx1, A_COLS], rb1.at[0], xn), (dw_ref.at[s, hy1, B_COLS], rb1.at[1], yn))
        elif phase == 2:
            pair = ((dw_ref.at[s, qa1, A_COLS], rb2.at[0], yn), (dw_ref.at[s, qb1, B_COLS], rb2.at[1], xn))
        elif phase == 3:
            pair = ((dwo.at[s, qa, A_COLS], dwo.at[s, qa, A_COLS], yn),
                    (dwo.at[s, qb, B_COLS], dwo.at[s, qb, B_COLS], xn))
        else:
            pair = ((dwo.at[s, hx, A_COLS], dwo.at[s, hx, A_COLS], xn),
                    (dwo.at[s, hy, B_COLS], dwo.at[s, hy, B_COLS], yn))
        return [rcopy(a, b, ws.at[phase - 1, i], wr.at[phase - 1, i], d) for i, (a, b, d) in enumerate(pair)]

    def w_start(phase, s):
        for cp in w_copy(phase, s):
            cp.start()

    def w_wait(phase, s):
        for cp in w_copy(phase, s):
            cp.wait()

    def add1(s):
        w_wait(1, s)
        dw_ref[s, hx, A_COLS] += rb1[0]
        dw_ref[s, hy, B_COLS] += rb1[1]

    def add2(s):
        w_wait(2, s)
        dwo[s, qa, A_COLS] = dw_ref[s, qa, A_COLS] + rb2[0]
        dwo[s, qb, B_COLS] = dw_ref[s, qb, B_COLS] + rb2[1]

    def w_final(s):
        slot = core * NS + s
        return (pltpu.make_async_copy(dwo.at[s], dw_out.at[slot], fl.at[s]),
                rcopy(dwo.at[s], dw_out.at[slot], fs.at[s], fr.at[s], partner))

    def deliver(s):
        w_wait(4, s)
        for cp in w_final(s):
            cp.start()

    def d1_copies(j):
        return (rcopy(dcr.at[j, oth_rows], rbd.at[j], d1s.at[0, j], d1r.at[0, j], partner),
                rcopy(drr.at[j, oth_rows], rbr.at[j], d1s.at[1, j], d1r.at[1, j], partner))

    def step(s, _):
        dw_ref[s] = jnp.zeros((LAT, 2 * GW), F32)
        for a in range(G):
            h = G * s + a
            qn[a] = qt[h].T
            dot_[a] = do_ref[h].T
        w_s = jnp.concatenate([wk[G * s + a] for a in range(G)] + [wv[G * s + a] for a in range(G)], axis=1)

        def phase1(j, stats, masked):
            rows = pl.ds(mul(j, CH), CH)
            kvv = nn(c_ref[rows, :], w_s).astype(BF16)
            kv[rows, :] = kvv
            rp = rn[rows, :]
            out = []
            for a in range(G):
                k_cat = jnp.concatenate([kvv[:, a * NOPE:(a + 1) * NOPE], rp], axis=1)
                s2 = nn(k_cat, qt[G * s + a]) * c2
                if masked:
                    ki = lax.broadcasted_iota(jnp.int32, (CH, CH), 0)
                    qi = lax.broadcasted_iota(jnp.int32, (CH, CH), 1)
                    s2 = jnp.where(ki <= qi, s2, -1e30)
                s_buf[a, rows, :] = s2
                cm = jnp.max(s2, axis=0, keepdims=True)
                if stats is None:
                    m = cm
                    l = jnp.sum(jnp.exp2(s2 - m), axis=0, keepdims=True)
                else:
                    m0, l0 = stats[a]
                    m = jnp.maximum(m0, cm)
                    l = l0 * jnp.exp2(m0 - m) + jnp.sum(jnp.exp2(s2 - m), axis=0, keepdims=True)
                out.append((m, l))
            return tuple(out)

        stats = phase1(chip, None, True)

        @pl.when(s == 0)
        def _():
            wait_latents()

        stats = lax.fori_loop(0, chip, lambda j, st: phase1(j, st, False), stats)
        lse = [m + jnp.log2(l) for m, l in stats]

        @pl.when(s > 1)
        def _():
            w_wait(3, s - 2)
            w_start(4, s - 2)

        def phase2(j, acc):
            rows = pl.ds(mul(j, CH), CH)
            out = []
            for a in range(G):
                pb = jnp.exp2(s_buf[a, rows, :] - lse[a]).astype(BF16)
                p_buf[a, rows, :] = pb
                v = kv[rows, GW + a * NOPE:GW + (a + 1) * NOPE]
                out.append(acc[a] + tn(v, pb))
            return tuple(out)

        ot = lax.fori_loop(0, chip + 1, phase2, tuple(jnp.zeros((NOPE, CH), F32) for _ in range(G)))
        delta = []
        for a in range(G):
            h = G * s + a
            delta.append(jnp.sum(ot[a] * dot_[a].astype(F32), axis=0, keepdims=True))
            o_ref[h] = ot[a].T.astype(BF16)

        @pl.when(s > 0)
        def _():
            add1(s - 1)
            w_start(2, s - 1)

        def phase3(j, acc):
            rows = pl.ds(mul(j, CH), CH)
            dks, dvs, out = [], [], []
            dr = jnp.zeros((CH, ROPE), F32)
            for a in range(G):
                h = G * s + a
                k = kv[rows, a * NOPE:(a + 1) * NOPE]
                v = kv[rows, GW + a * NOPE:GW + (a + 1) * NOPE]
                pb = p_buf[a, rows, :]
                dp = nn(v, dot_[a])
                ds = (pb.astype(F32) * (dp - delta[a])).astype(BF16)
                out.append((acc[a][0] + tn(k, ds), acc[a][1] + nn(rt[:, rows], ds)))
                dkr = nn(ds, qn[a]) * scale
                dks.append(dkr[:, :NOPE].astype(BF16))
                dr = dr + dkr[:, NOPE:]
                dvs.append(nn(pb, do_ref[h]).astype(BF16))
            dkv = jnp.concatenate(dks + dvs, axis=1)
            drr[j] += dr
            dcr[j] += nt(dkv, w_s)
            dw_ref[s] += nn(ct[j], dkv)

            @pl.when(s == NS - 1)
            def _():
                for cp in d1_copies(j):
                    cp.start()
            return tuple(out)

        dqt = lax.fori_loop(0, chip + 1, phase3, tuple((jnp.zeros((NOPE, CH), F32), jnp.zeros((ROPE, CH), F32)) for _ in range(G)))
        for a in range(G):
            dq_ref[G * s + a, :NOPE] = (dqt[a][0] * scale).astype(BF16)
            dq_ref[G * s + a, NOPE:] = (dqt[a][1] * scale).astype(BF16)

        @pl.when(s > 0)
        def _():
            add2(s - 1)

        @pl.when(s > 1)
        def _():
            deliver(s - 2)

        @pl.when(s > 0)
        def _():
            w_start(3, s - 1)

        w_start(1, s)
        return 0

    lax.fori_loop(0, NS, step, 0)

    outs = [pltpu.make_async_copy(o_ref.at[:, own_rows], o_out.at[mine], lsem.at[6]),
            pltpu.make_async_copy(dq_ref.at[:, :, own_rows], dq_out.at[mine], lsem.at[7]),
            rcopy(o_ref.at[:, oth_rows], o_out.at[mine], xs.at[2], xr.at[2], partner),
            rcopy(dq_ref.at[:, :, oth_rows], dq_out.at[mine], xs.at[3], xr.at[3], partner)]
    for cp in outs:
        cp.start()

    def join(j, _):
        for cp in d1_copies(j):
            cp.wait()
        msg[j, :TOK] = dcr[j, own_rows, :] + rbd[j]
        drt = (drr[j, own_rows, :] + rbr[j]).T
        msg[j, TOK:] = jnp.concatenate([drt[:ROPE // 2], drt[ROPE // 2:]], axis=1)
        return 0
    lax.fori_loop(0, chip + 1, join, 0)

    first, second = pl.ds(0, MSG // 2), pl.ds(MSG // 2, MSG // 2)
    sends = ((chip_x, rcopy(msg.at[chip_x], rbe.at[0], d2s.at[0], d2r.at[0], xn)),
             (chip_y, rcopy(msg.at[chip_y], rbe.at[1], d2s.at[1], d2r.at[1], yn)),
             (chip_d, rcopy(msg.at[chip_d, first], rbe.at[2, first], d2s.at[2], d2r.at[2], dn)),
             (chip_d, rcopy(msg.at[chip_d, second], rly, d2s.at[3], d2r.at[3], yn)))
    relay = rcopy(rly, rbe.at[2, second], d2s.at[4], d2r.at[4], xn)
    low = y == 0

    w_wait(3, NS - 2)
    w_start(4, NS - 2)
    for i in (3, 2):
        @pl.when(sends[i][0] < chip)
        def _(i=i):
            sends[i][1].start()
    add1(NS - 1)
    w_start(2, NS - 1)
    for i in (0, 1):
        @pl.when(sends[i][0] < chip)
        def _(i=i):
            sends[i][1].start()

    @pl.when(low)
    def _():
        sends[3][1].wait_recv()
        relay.start()
    add2(NS - 1)
    deliver(NS - 2)
    w_start(3, NS - 1)
    w_wait(3, NS - 1)
    w_start(4, NS - 1)
    for i in (0, 1):
        @pl.when(sends[i][0] > chip)
        def _(i=i):
            sends[i][1].wait_recv()
            msg[chip] += rbe[i]

    @pl.when(low)
    def _():
        sends[2][1].wait_recv()
        relay.wait_recv()
        msg[chip] += rbe[2]
        relay.wait_send()
    for ch, cp in sends:
        @pl.when(ch < chip)
        def _(cp=cp):
            cp.wait_send()
    dlat_out[...] = msg[chip, :TOK].astype(BF16)
    dr_out[:ROPE // 2] = msg[chip, TOK:, :TOK].astype(BF16)
    dr_out[ROPE // 2:] = msg[chip, TOK:, TOK:].astype(BF16)
    deliver(NS - 1)
    for cp in outs:
        cp.wait()

    def drain(s, _):
        for cp in w_final(s):
            cp.wait()
        return 0
    lax.fori_loop(0, NS, drain, 0)


PARTS = 4


def layout_kernel(o_t, dw, o_ref, dk_ref, dv_ref, stage):
    tok, lat = TOK // PARTS, LAT // PARTS
    for h in range(HEADS):
        stage[pl.ds(h, tok, stride=HEADS), :] = o_t[h].astype(F32)
    o_ref[...] = stage[...].astype(BF16)
    for i in range(2 * NS):
        for a in range(G):
            rows = pl.ds(G * i + a, lat, stride=HEADS)
            dk_ref[rows, :] = dw[i, :, a * NOPE:(a + 1) * NOPE]
            dv_ref[rows, :] = dw[i, :, GW + a * NOPE:GW + (a + 1) * NOPE]


def to_output_layout(o_t, dw):
    tok, lat = TOK // PARTS, LAT // PARTS
    return pl.pallas_call(
        layout_kernel,
        grid=(PARTS,),
        out_shape=(jax.ShapeDtypeStruct((TOK * HEADS, NOPE), BF16),
                   jax.ShapeDtypeStruct((LAT * HEADS, NOPE), F32),
                   jax.ShapeDtypeStruct((LAT * HEADS, NOPE), F32)),
        in_specs=[pl.BlockSpec((HEADS, tok, NOPE), lambda i: (0, i, 0)),
                  pl.BlockSpec((2 * NS, lat, 2 * GW), lambda i: (0, i, 0))],
        out_specs=[pl.BlockSpec((tok * HEADS, NOPE), lambda i: (i, 0)),
                   pl.BlockSpec((lat * HEADS, NOPE), lambda i: (i, 0)),
                   pl.BlockSpec((lat * HEADS, NOPE), lambda i: (i, 0))],
        scratch_shapes=[pltpu.VMEM((tok * HEADS, NOPE), F32)],
        compiler_params=pltpu.CompilerParams(vmem_limit_bytes=60 << 20),
    )(o_t, dw)


def solution(mesh):
    seq_spec = P("cp")

    def local_step(queries, latent, key_rope, w_uk, w_uv, d_out):
        any_spec = pl.BlockSpec(memory_space=pl.ANY)
        vm_spec = pl.BlockSpec(memory_space=pltpu.VMEM)
        dma = pltpu.SemaphoreType.DMA
        vm = pltpu.VMEM
        o_t, dq_t, dw, d_latent, d_key_rope = pl.pallas_call(
            attn_kernel,
            out_shape=(jax.ShapeDtypeStruct((HEADS, TOK, NOPE), BF16),
                       jax.ShapeDtypeStruct((HEADS, QK, TOK), BF16),
                       jax.ShapeDtypeStruct((2 * NS, LAT, 2 * GW), F32),
                       jax.ShapeDtypeStruct((TOK, LAT), BF16),
                       jax.ShapeDtypeStruct((ROPE, TOK), BF16)),
            in_specs=[any_spec] * 6,
            out_specs=[any_spec] * 3 + [vm_spec] * 2,
            scratch_shapes=[vm((TOK * HEADS, NOPE), BF16),
                            vm((LAT, HPC, NOPE), BF16), vm((LAT, HPC, NOPE), BF16),
                            vm((TOK * HEADS, NOPE), F32), vm((HPC, TOK, NOPE), BF16),
                            vm((HPC, QK, CH), BF16), vm((HPC, CH, NOPE), BF16),
                            vm((SEQ, LAT), BF16), vm((ROPE, SEQ), BF16), vm((SEQ, ROPE), BF16),
                            vm((HPC, LAT, NOPE), BF16), vm((HPC, LAT, NOPE), BF16),
                            vm((HPC, CH, NOPE), BF16), vm((HPC, QK, CH), BF16),
                            vm((NS, LAT, 2 * GW), F32), vm((NS, LAT, 2 * GW), F32),
                            vm((NCHIP, CH, LAT), F32), vm((NCHIP, CH, ROPE), F32), vm((NCHIP, MSG, LAT), F32),
                            vm((NCHIP, LAT, CH), BF16), vm((SEQ, 2 * GW), BF16),
                            vm((G, CH, QK), BF16), vm((G, NOPE, CH), BF16),
                            vm((G, SEQ, CH), F32), vm((G, SEQ, CH), BF16),
                            vm((2, 256, GW), F32), vm((2, 128, GW), F32),
                            vm((NCHIP, TOK, LAT), F32), vm((NCHIP, TOK, ROPE), F32),
                            vm((3, MSG, LAT), F32), vm((MSG // 2, LAT), F32),
                            dma((8,)), dma((4,)), dma((4,)), dma((2, 7)), dma((2, 7)),
                            dma((4, 2)), dma((4, 2)), dma((NS,)), dma((NS,)), dma((NS,)),
                            dma((2, NCHIP)), dma((2, NCHIP)), dma((5,)), dma((5,))],
            compiler_params=pltpu.CompilerParams(vmem_limit_bytes=63 << 20, collective_id=0, has_side_effects=True),
            cost_estimate=pl.CostEstimate(flops=30 * 10**9, bytes_accessed=20 << 20, transcendentals=10**7),
        )(jnp.transpose(queries, (1, 2, 0)), d_out.reshape(TOK * HEADS, NOPE), latent, key_rope.T, w_uk, w_uv)

        o, dk, dv = to_output_layout(o_t, dw)
        return (o.reshape(TOK, HEADS, NOPE), jnp.transpose(dq_t, (2, 0, 1)), d_latent, d_key_rope.T,
                dk.reshape(LAT, HEADS, NOPE), dv.reshape(LAT, HEADS, NOPE))

    return jax.shard_map(local_step, mesh=mesh,
                         in_specs=(seq_spec, seq_spec, seq_spec, P(), P(), seq_spec),
                         out_specs=(seq_spec, seq_spec, seq_spec, seq_spec, P(), P()),
                         check_vma=False)
```

time: 208 us -> 160 us (0.77)
  local copies, waits for them, and re-layouts: 44 us -> 2.47 us
  Pallas kernels: 161 us -> 156 us
    slice x3 -> x0, local copies, waits for them, and re-layouts: 15.1 us -> none  [local_step(): return (attn_out, d_query, d_latent, d_key_rope, dw[0], dw[1])]
    unnamed x17 -> x9, local copies, waits for them, and re-layouts: 15.2 us -> 2.47 us
    reshape x1 -> x0, local copies, waits for them, and re-layouts: 10.5 us -> none  [local_step(): dw = dw.reshape(2 * NS, LAT, 2, 2, NOPE)]
    pallas_call x1 -> x2, Pallas kernels: 161 us -> 156 us  [the longest x1 146 us: local_step(): pl.pallas_call(attn_kernel, out_shape=(jax.ShapeDtypeStruct((HEADS, TOK,...]
where the time goes in v3:
time: 160 us
  Pallas kernels  156 us (98%)
  local copies, waits for them, and re-layouts  2.47 us (2%)
    pallas_call x1, Pallas kernels, local_step(): pl.pallas_call(attn_kernel, out_shape=(jax.ShapeDtypeStruct((HEADS, TOK,...  146 us
    pallas_call x1, Pallas kernels, to_output_layout(): pl.pallas_call(layout_kernel, grid=(PARTS,), out_shape=(jax.ShapeDtypeStr...  9.91 us

profile of v3, /device:TPU:0, one launch (start us, length us, event | category | flops | bytes accessed | tf_op | source)
XLA Modules:
  0.0 159.5 jit_solution(4997347690075761743)
XLA Ops:
  0.6 146.5 %shard_map.109 = (bf16[16,256,128]{2,1,0:T(8,128)(2,1)}, bf16[16,192,256]{2,1,0:T(8,128)(2,1)}, f32[8,512,512]{2,1,0:T(8,128)}, bf16[256,512]{1,0:T(8,128)(2,1)}, bf16[64,256]{1,0:T(8,128)(2,1)}) custom-call(bf16[16,192,256]{2,1,0:T(8,128)(2,1)} %bitcast.12, bf16[4096,128]{1,0:T(8,128)(2,1)} %bitcast.13, bf16[256,512]{1,0:T(8,128)(2,1)} %c_in.1, ...), custom_call_target="tpu_custom_call" | custom-call | flops 30000001024 | bytes 20971520 | tf_op jit(solution)/shard_map/pallas_call | solution.py:456
  147.1 0.0 copy-start
  147.1 9.9 %shard_map.110 = (bf16[4096,128]{1,0:T(8,128)(2,1)}, f32[8192,128]{1,0:T(8,128)}, f32[8192,128]{1,0:T(8,128)}) custom-call(bf16[16,256,128]{2,1,0:T(8,128)(2,1)} %get-tuple-element.14.o_t, f32[8,512,512]{2,1,0:T(8,128)} %get-tuple-element.15.dw), custom_call_target="tpu_custom_call" | custom-call | tf_op jit(solution)/shard_map/pallas_call | solution.py:432
  157.0 0.0 copy-start.1
  157.0 0.0 copy-start.2
  157.0 0.0 copy-done
  157.0 1.1 copy.15
  158.2 0.0 copy-done.1
  158.2 0.7 copy.16
  158.9 0.0 copy-done.2
  158.9 0.6 copy.17
Async XLA Ops:
  147.1 9.9 %copy-start = (bf16[16,192,256]{2,1,0:T(8,128)(2,1)S(1)}, bf16[16,192,256]{2,1,0:T(8,128)(2,1)}, u32[]{:S(2)}) copy-start(bf16[16,192,256]{2,1,0:T(8,128)(2,1)} %get-tuple-element.17) | copy-start | bytes 4718596
  157.0 1.2 copy-start.1
  157.0 1.9 %copy-start.2 = (bf16[64,256]{1,0:T(8,128)(2,1)S(1)}, bf16[64,256]{1,0:T(8,128)(2,1)}, u32[]{:S(2)}) copy-start(bf16[64,256]{1,0:T(8,128)(2,1)} %get-tuple-element.19) | copy-start | bytes 98308

commit v4 on v3

v4 whole, which is shorter than its diff:
```python
import math
import jax
import jax.numpy as jnp
from jax import lax
from jax.experimental import pallas as pl
from jax.experimental.pallas import tpu as pltpu
from jax.sharding import PartitionSpec as P

F32 = jnp.float32
BF16 = jnp.bfloat16
TOK = 256
CH = 512
KC = 1024
HEADS = 16
HPC = 8
NS = HPC
NOPE = 128
ROPE = 64
QK = NOPE + ROPE
LAT = 512
MSG = TOK + ROPE // 2
NCHIP = 4
SEQ = CH * NCHIP
MESH = pl.DeviceIdType.MESH
A_COLS = pl.ds(0, NOPE)
B_COLS = pl.ds(NOPE, NOPE)


def nt(a, b):
    return lax.dot_general(a, b, (((1,), (1,)), ((), ())), preferred_element_type=F32)


def nn(a, b):
    return lax.dot_general(a, b, (((1,), (0,)), ((), ())), preferred_element_type=F32)


def tn(a, b):
    return lax.dot_general(a, b, (((0,), (0,)), ((), ())), preferred_element_type=F32)


def mul(i, n):
    return pl.multiple_of(i * n, n)


def attn_kernel(q_in, do_in, c_in, r_in, wk_in, wv_in,
                o_out, dq_out, dw_out, dlat_out, dr_out,
                do_raw, wk_raw, wv_raw, stage, do_snd,
                qt, do_ref, c_ref, rt, rn, wk, wv, o_ref, dq_ref, dw_ref, dwo, dcr, drr, msg,
                ct, kv, qn, dot_, s_buf, p_buf, rb1, rb2, rbd, rbr, rbx, rby, rbh,
                lsem, xs, xr, cs, crs, ws, wr, fs, fr, fl, d1s, d1r, d2s, d2r):
    scale = 1.0 / math.sqrt(QK)
    c2 = scale * math.log2(math.e)
    me = lax.axis_index("cp")
    core = lax.rem(me, 2)
    chip = lax.div(me, 2)
    x = lax.rem(chip, 2)
    y = lax.div(chip, 2)
    partner = me + 1 - 2 * core
    xn = me + 2 - 4 * x
    yn = me + 4 - 8 * y
    dn = xn + 4 - 8 * y

    def rcopy(src, dst, ss, rs, dev):
        return pltpu.make_async_remote_copy(src_ref=src, dst_ref=dst, send_sem=ss, recv_sem=rs,
                                            device_id=(dev,), device_id_type=MESH)

    my_rows = pl.ds(mul(me, TOK), TOK)
    own_rows = pl.ds(mul(core, TOK), TOK)
    oth_rows = pl.ds(mul(1 - core, TOK), TOK)
    mine = pl.ds(mul(core, HPC), HPC)

    other = pl.ds(mul(1 - core, HPC), HPC)

    local = [pltpu.make_async_copy(c_in, c_ref.at[my_rows], lsem.at[0]),
             pltpu.make_async_copy(r_in, rt.at[:, my_rows], lsem.at[1]),
             pltpu.make_async_copy(q_in.at[mine], qt.at[:, :, own_rows], lsem.at[2]),
             pltpu.make_async_copy(do_in, do_raw, lsem.at[3]),
             pltpu.make_async_copy(wk_in.at[:, mine], wk_raw, lsem.at[4]),
             pltpu.make_async_copy(wv_in.at[:, mine], wv_raw, lsem.at[5])]
    for cp in local:
        cp.start()

    bar = pltpu.get_barrier_semaphore()
    for peer in (partner, xn, yn, dn):
        pl.semaphore_signal(bar, inc=1, device_id=(peer,), device_id_type=MESH)
    pl.semaphore_wait(bar, 4)

    local[0].wait()
    local[1].wait()

    def latent_copies(i, src, dev):
        rows = pl.ds(mul(src, TOK), TOK)
        return (rcopy(c_ref.at[rows], c_ref.at[rows], cs.at[0, i], crs.at[0, i], dev),
                rcopy(rt.at[:, rows], rt.at[:, rows], cs.at[1, i], crs.at[1, i], dev))

    c_direct = [latent_copies(i, me, dev) for i, dev in enumerate((partner, xn, yn, dn))]
    for pair in c_direct:
        for cp in pair:
            cp.start()

    heads = [rcopy(q_in.at[other], qt.at[:, :, own_rows], xs.at[0], xr.at[0], partner),
             rcopy(do_snd, do_ref.at[:, own_rows], xs.at[1], xr.at[1], partner)]
    heads[0].start()
    local[3].wait()

    def pick(h, rows, stride):
        return stage[pl.ds(h, rows, stride=stride), :].astype(BF16)

    def widen(i, _):
        rows = pl.ds(mul(i, 256), 256)
        stage[rows, :] = do_raw[rows, :].astype(F32)
        return 0
    lax.fori_loop(0, TOK * HEADS // 256, widen, 0)
    is0 = core == 0
    for i in range(HPC):
        lo = pick(i, TOK, HEADS)
        hi = pick(i + HPC, TOK, HEADS)
        do_ref[i, own_rows, :] = jnp.where(is0, lo, hi)
        do_snd[i] = jnp.where(is0, hi, lo)
    heads[1].start()
    for t, (raw, out) in enumerate(((wk_raw, wk), (wv_raw, wv))):
        local[4 + t].wait()

        def body(i, _, raw=raw):
            ls = pl.ds(mul(i, 32), 32)
            stage[pl.ds(mul(i, 256), 256), :] = raw[ls].astype(F32).reshape(256, NOPE)
            return 0
        lax.fori_loop(0, LAT // 32, body, 0)
        for i in range(HPC):
            out[i] = pick(i, LAT, HPC)

    def zero_dc(j, _):
        rows = pl.ds(mul(j, KC), KC)
        dcr[rows, :] = jnp.zeros((KC, LAT), F32)
        drr[rows, :] = jnp.zeros((KC, ROPE), F32)
        return 0
    lax.fori_loop(0, y + 1, zero_dc, 0)
    local[2].wait()
    for cp in heads:
        cp.wait()
    for cp in c_direct[0]:
        cp.wait()

    def turn(j):
        rows = pl.ds(mul(j, KC), KC)
        ct[j] = c_ref[rows, :].T
        rn[rows, :] = rt[:, rows].T

    c_fwd = [None] + [latent_copies(3 + i, src, partner) for i, src in ((1, xn), (2, yn), (3, dn))]

    def wait_latents(which):
        for i in which:
            for cp in c_direct[i]:
                cp.wait()
            for cp in c_fwd[i]:
                cp.start()
        for i in which:
            for cp in c_fwd[i]:
                cp.wait()

    wait_latents((1,))
    turn(y)

    hx = pl.ds(mul(x, 256), 256)
    hx1 = pl.ds(mul(1 - x, 256), 256)
    hy = pl.ds(mul(y, 256), 256)
    hy1 = pl.ds(mul(1 - y, 256), 256)
    qa = pl.ds(pl.multiple_of(x * 256 + y * 128, 128), 128)
    qa1 = pl.ds(pl.multiple_of(x * 256 + (1 - y) * 128, 128), 128)
    qb = pl.ds(pl.multiple_of(y * 256 + x * 128, 128), 128)
    qb1 = pl.ds(pl.multiple_of(y * 256 + (1 - x) * 128, 128), 128)

    def w_copy(phase, s):
        par = lax.rem(s, 2)
        if phase == 1:
            pair = ((dw_ref.at[s, hx1, A_COLS], rb1.at[par, 0], xn), (dw_ref.at[s, hy1, B_COLS], rb1.at[par, 1], yn))
        elif phase == 2:
            pair = ((dw_ref.at[s, qa1, A_COLS], rb2.at[par, 0], yn), (dw_ref.at[s, qb1, B_COLS], rb2.at[par, 1], xn))
        elif phase == 3:
            pair = ((dwo.at[s, qa, A_COLS], dwo.at[s, qa, A_COLS], yn),
                    (dwo.at[s, qb, B_COLS], dwo.at[s, qb, B_COLS], xn))
        else:
            pair = ((dwo.at[s, hx, A_COLS], dwo.at[s, hx, A_COLS], xn),
                    (dwo.at[s, hy, B_COLS], dwo.at[s, hy, B_COLS], yn))
        return [rcopy(a, b, ws.at[phase - 1, par, i], wr.at[phase - 1, par, i], d)
                for i, (a, b, d) in enumerate(pair)]

    def w_start(phase, s):
        for cp in w_copy(phase, s):
            cp.start()

    def w_wait(phase, s):
        for cp in w_copy(phase, s):
            cp.wait()

    def w_final(s, late):
        slot = core * NS + s
        parts = ((hx1, A_COLS), (hy1, B_COLS)) if late else ((hx, A_COLS), (hy, B_COLS))
        return [rcopy(dwo.at[s, r, c], dw_out.at[slot, r, c], fs.at[s, 2 * late + i], fr.at[s, 2 * late + i], partner)
                for i, (r, c) in enumerate(parts)]

    def w_local(s):
        return pltpu.make_async_copy(dwo.at[s], dw_out.at[core * NS + s], fl.at[s])

    def stage2(s):
        par = lax.rem(s, 2)
        w_wait(1, s)
        dw_ref[s, hx, A_COLS] += rb1[par, 0]
        dw_ref[s, hy, B_COLS] += rb1[par, 1]
        w_start(2, s)

    def stage3(s):
        par = lax.rem(s, 2)
        w_wait(2, s)
        dwo[s, qa, A_COLS] = dw_ref[s, qa, A_COLS] + rb2[par, 0]
        dwo[s, qb, B_COLS] = dw_ref[s, qb, B_COLS] + rb2[par, 1]
        w_start(3, s)

    def stage4(s):
        w_wait(3, s)
        w_start(4, s)
        for cp in w_final(s, 0):
            cp.start()

    def stage5(s):
        w_wait(4, s)
        for cp in w_final(s, 1):
            cp.start()
        w_local(s).start()

    def d1_copies(j):
        rows = pl.ds(pl.multiple_of(j * CH + (1 - core) * TOK, TOK), TOK)
        return (rcopy(dcr.at[rows], rbd.at[j], d1s.at[0, j], d1r.at[0, j], partner),
                rcopy(drr.at[rows], rbr.at[j], d1s.at[1, j], d1r.at[1, j], partner))

    def step(s, _):
        dw_ref[s] = jnp.zeros((LAT, 2 * NOPE), F32)
        qn[...] = qt[s].T
        dot_[...] = do_ref[s].T
        w_s = jnp.concatenate([wk[s], wv[s]], axis=1)

        def phase1(j, masked):
            rows = pl.ds(mul(j, KC), KC)
            kvv = nn(c_ref[rows, :], w_s).astype(BF16)
            kv[rows, :] = kvv
            k_cat = jnp.concatenate([kvv[:, :NOPE], rn[rows, :]], axis=1)
            s2 = nn(k_cat, qt[s]) * c2
            if masked:
                ki = lax.broadcasted_iota(jnp.int32, (KC, CH), 0)
                qi = lax.broadcasted_iota(jnp.int32, (KC, CH), 1)
                s2 = jnp.where(ki - qi <= x * CH, s2, -1e30)
            s_buf[rows, :] = s2
            m = jnp.max(s2, axis=0, keepdims=True)
            return m, jnp.sum(jnp.exp2(s2 - m), axis=0, keepdims=True)

        stats = phase1(y, True)

        @pl.when(s == 0)
        def _():
            @pl.when(y == 1)
            def _():
                wait_latents((2, 3))
                turn(0)

        def more(j, st):
            m0, l0 = st
            m1, l1 = phase1(j, False)
            m = jnp.maximum(m0, m1)
            return m, l0 * jnp.exp2(m0 - m) + l1 * jnp.exp2(m1 - m)

        m, l = lax.fori_loop(0, y, more, stats)
        lse = m + jnp.log2(l)

        def phase2(j, acc):
            rows = pl.ds(mul(j, KC), KC)
            pb = jnp.exp2(s_buf[rows, :] - lse).astype(BF16)
            p_buf[rows, :] = pb
            return acc + tn(kv[rows, NOPE:], pb)

        ot = lax.fori_loop(0, y + 1, phase2, jnp.zeros((NOPE, CH), F32))
        delta = jnp.sum(ot * dot_[...].astype(F32), axis=0, keepdims=True)
        o_ref[s] = ot.T.astype(BF16)

        @pl.when(s > 1)
        def _():
            stage3(s - 2)

        def phase3(j, acc):
            rows = pl.ds(mul(j, KC), KC)
            k = kv[rows, :NOPE]
            v = kv[rows, NOPE:]
            pb = p_buf[rows, :]
            dp = nn(v, dot_[...])
            ds = (pb.astype(F32) * (dp - delta)).astype(BF16)
            dkr = nn(ds, qn[...]) * scale
            dv = nn(pb, do_ref[s])
            dkv = jnp.concatenate([dkr[:, :NOPE].astype(BF16), dv.astype(BF16)], axis=1)
            drr[rows, :] += dkr[:, NOPE:]
            dcr[rows, :] += nt(dkv, w_s)
            dw_ref[s] += nn(ct[j], dkv)
            out = (acc[0] + tn(k, ds), acc[1] + nn(rt[:, rows], ds))

            @pl.when(s == NS - 1)
            def _():
                for t in range(2):
                    for cp in d1_copies(2 * j + t):
                        cp.start()

            @pl.when(j == 0)
            def _():
                @pl.when(s > 0)
                def _():
                    stage2(s - 1)
            return out

        dqn, dqr = lax.fori_loop(0, y + 1, phase3, (jnp.zeros((NOPE, CH), F32), jnp.zeros((ROPE, CH), F32)))
        w_start(1, s)
        dq_ref[s, :NOPE] = (dqn * scale).astype(BF16)
        dq_ref[s, NOPE:] = (dqr * scale).astype(BF16)

        @pl.when(s > 1)
        def _():
            stage4(s - 2)

        @pl.when(s > 2)
        def _():
            stage5(s - 3)
        return 0

    lax.fori_loop(0, NS, step, 0)

    @pl.when(y == 0)
    def _():
        wait_latents((2, 3))

    outs = [pltpu.make_async_copy(o_ref.at[:, own_rows], o_out.at[mine], lsem.at[6]),
            pltpu.make_async_copy(dq_ref.at[:, :, own_rows], dq_out.at[mine], lsem.at[7]),
            rcopy(o_ref.at[:, oth_rows], o_out.at[mine], xs.at[2], xr.at[2], partner),
            rcopy(dq_ref.at[:, :, oth_rows], dq_out.at[mine], xs.at[3], xr.at[3], partner)]
    for cp in outs:
        cp.start()

    def join(j):
        for cp in d1_copies(j):
            cp.wait()
        rows = pl.ds(pl.multiple_of(j * CH + core * TOK, TOK), TOK)
        msg[j, :TOK] = dcr[rows, :] + rbd[j]
        drt = (drr[rows, :] + rbr[j]).T
        msg[j, TOK:] = jnp.concatenate([drt[:ROPE // 2], drt[ROPE // 2:]], axis=1)


    halves = (pl.ds(0, MSG // 2), pl.ds(MSG // 2, MSG // 2))

    def to_x(j):
        return [rcopy(msg.at[j, h], rbx.at[h], d2s.at[0, i], d2r.at[0, i], xn) for i, h in enumerate(halves)]

    def to_y(j):
        return [rcopy(msg.at[j, h], rby.at[h], d2s.at[1, i], d2r.at[1, i], yn) for i, h in enumerate(halves)]

    half_x = rcopy(msg.at[0, halves[0]], rbh, d2s.at[2, 0], d2r.at[2, 0], xn)
    half_y = rcopy(msg.at[0, halves[1]], rbh, d2s.at[2, 1], d2r.at[2, 0], yn)

    stage3(NS - 2)
    join(0)
    stage2(NS - 1)

    @pl.when(chip == 3)
    def _():
        half_x.start()
        half_y.start()
    join(1)

    @pl.when(chip == 2)
    def _():
        for cp in to_x(1):
            cp.start()
    stage5(NS - 3)

    @pl.when(y == 1)
    def _():
        join(2)
    stage4(NS - 2)
    stage3(NS - 1)

    @pl.when(chip == 2)
    def _():
        half_x.wait_recv()
        msg[0, halves[0]] += rbh[...]

    @pl.when(chip == 1)
    def _():
        half_y.wait_recv()
        msg[0, halves[1]] += rbh[...]
    stage4(NS - 1)

    @pl.when(chip == 1)
    def _():
        for cp in to_x(0):
            cp.start()

    @pl.when(chip == 2)
    def _():
        for cp in to_y(0):
            cp.start()

    @pl.when(chip == 3)
    def _():
        for cp in to_x(2):
            cp.start()
        for i, h in enumerate(halves):
            to_x(1)[i].wait_recv()
            msg[1, h] += rbx[h]
            to_y(1)[i].start()

    @pl.when(y == 1)
    def _():
        join(3)
    stage5(NS - 2)
    stage5(NS - 1)

    def all_of(copies, recv):
        for cp in copies:
            if recv:
                cp.wait_recv()
            else:
                cp.wait_send()

    @pl.when(chip != 3)
    def _():
        @pl.when(chip != 1)
        def _():
            all_of(to_x(0), True)
            msg[chip] += rbx[...]

        @pl.when(chip != 2)
        def _():
            all_of(to_y(0), True)
            msg[chip] += rby[...]

    dlat_out[...] = msg[chip, :TOK].astype(BF16)
    dr_out[:ROPE // 2] = msg[chip, TOK:, :TOK].astype(BF16)
    dr_out[ROPE // 2:] = msg[chip, TOK:, TOK:].astype(BF16)

    @pl.when(chip != 0)
    def _():
        all_of(to_x(0), False)

        @pl.when(chip != 1)
        def _():
            all_of(to_y(0), False)

    @pl.when(chip == 3)
    def _():
        all_of((half_x, half_y), False)
    for cp in outs:
        cp.wait()

    def drain(s, _):
        for cp in w_final(s, 0) + w_final(s, 1):
            cp.wait()
        w_local(s).wait()
        return 0
    lax.fori_loop(0, NS, drain, 0)


PARTS = 2


def layout_kernel(o_t, dw, dq_t, dc, dr, o_ref, dk_ref, dv_ref, dq_ref, dc_ref, dr_ref):
    def by_row(v):
        return jnp.swapaxes(v, 0, 1).reshape(v.shape[0] * v.shape[1], NOPE)

    dk_ref[...] = by_row(dw[:, :, :NOPE])
    dv_ref[...] = by_row(dw[:, :, NOPE:])
    o_ref[...] = by_row(o_t[...].astype(F32)).astype(BF16)
    dq_ref[...] = dq_t[...]
    dc_ref[...] = dc[...]
    dr_ref[...] = dr[...]


def to_output_layout(o_t, dw, dq_t, dc, dr):
    tok, lat = TOK // PARTS, LAT // PARTS
    passed = [pl.BlockSpec((HEADS // PARTS, QK, TOK), lambda i: (i, 0, 0)),
              pl.BlockSpec((tok, LAT), lambda i: (i, 0)),
              pl.BlockSpec((ROPE // PARTS, TOK), lambda i: (i, 0))]
    return pl.pallas_call(
        layout_kernel,
        grid=(PARTS,),
        out_shape=(jax.ShapeDtypeStruct((TOK * HEADS, NOPE), BF16),
                   jax.ShapeDtypeStruct((LAT * HEADS, NOPE), F32),
                   jax.ShapeDtypeStruct((LAT * HEADS, NOPE), F32),
                   jax.ShapeDtypeStruct(dq_t.shape, BF16),
                   jax.ShapeDtypeStruct(dc.shape, BF16),
                   jax.ShapeDtypeStruct(dr.shape, BF16)),
        in_specs=[pl.BlockSpec((HEADS, tok, NOPE), lambda i: (0, i, 0)),
                  pl.BlockSpec((HEADS, lat, 2 * NOPE), lambda i: (0, i, 0))] + passed,
        out_specs=[pl.BlockSpec((tok * HEADS, NOPE), lambda i: (i, 0)),
                   pl.BlockSpec((lat * HEADS, NOPE), lambda i: (i, 0)),
                   pl.BlockSpec((lat * HEADS, NOPE), lambda i: (i, 0))] + passed,
        compiler_params=pltpu.CompilerParams(vmem_limit_bytes=60 << 20),
    )(o_t, dw, dq_t, dc, dr)


def solution(mesh):
    seq_spec = P("cp")

    def local_step(queries, latent, key_rope, w_uk, w_uv, d_out):
        any_spec = pl.BlockSpec(memory_space=pl.ANY)
        vm_spec = pl.BlockSpec(memory_space=pltpu.VMEM)
        dma = pltpu.SemaphoreType.DMA
        vm = pltpu.VMEM
        o_t, dq_t, dw, d_latent, d_key_rope = pl.pallas_call(
            attn_kernel,
            out_shape=(jax.ShapeDtypeStruct((HEADS, TOK, NOPE), BF16),
                       jax.ShapeDtypeStruct((HEADS, QK, TOK), BF16),
                       jax.ShapeDtypeStruct((HEADS, LAT, 2 * NOPE), F32),
                       jax.ShapeDtypeStruct((TOK, LAT), BF16),
                       jax.ShapeDtypeStruct((ROPE, TOK), BF16)),
            in_specs=[any_spec] * 6,
            out_specs=[any_spec] * 3 + [vm_spec] * 2,
            scratch_shapes=[vm((TOK * HEADS, NOPE), BF16),
                            vm((LAT, HPC, NOPE), BF16), vm((LAT, HPC, NOPE), BF16),
                            vm((TOK * HEADS, NOPE), F32), vm((HPC, TOK, NOPE), BF16),
                            vm((HPC, QK, CH), BF16), vm((HPC, CH, NOPE), BF16),
                            vm((SEQ, LAT), BF16), vm((ROPE, SEQ), BF16), vm((SEQ, ROPE), BF16),
                            vm((HPC, LAT, NOPE), BF16), vm((HPC, LAT, NOPE), BF16),
                            vm((HPC, CH, NOPE), BF16), vm((HPC, QK, CH), BF16),
                            vm((NS, LAT, 2 * NOPE), F32), vm((NS, LAT, 2 * NOPE), F32),
                            vm((SEQ, LAT), F32), vm((SEQ, ROPE), F32), vm((NCHIP, MSG, LAT), F32),
                            vm((SEQ // KC, LAT, KC), BF16), vm((SEQ, 2 * NOPE), BF16),
                            vm((CH, QK), BF16), vm((NOPE, CH), BF16),
                            vm((SEQ, CH), F32), vm((SEQ, CH), BF16),
                            vm((2, 2, 256, NOPE), F32), vm((2, 2, 128, NOPE), F32),
                            vm((NCHIP, TOK, LAT), F32), vm((NCHIP, TOK, ROPE), F32),
                            vm((MSG, LAT), F32), vm((MSG, LAT), F32), vm((MSG // 2, LAT), F32),
                            dma((8,)), dma((4,)), dma((4,)), dma((2, 7)), dma((2, 7)),
                            dma((4, 2, 2)), dma((4, 2, 2)), dma((NS, 4)), dma((NS, 4)), dma((NS,)),
                            dma((2, NCHIP)), dma((2, NCHIP)), dma((3, 2)), dma((3, 2))],
            compiler_params=pltpu.CompilerParams(vmem_limit_bytes=63 << 20, collective_id=0, has_side_effects=True),
            cost_estimate=pl.CostEstimate(flops=30 * 10**9, bytes_accessed=20 << 20, transcendentals=10**7),
        )(jnp.transpose(queries, (1, 2, 0)), d_out.reshape(TOK * HEADS, NOPE), latent, key_rope.T, w_uk, w_uv)

        o, dk, dv, dq_t, d_latent, d_key_rope = to_output_layout(o_t, dw, dq_t, d_latent, d_key_rope)
        return (o.reshape(TOK, HEADS, NOPE), jnp.transpose(dq_t, (2, 0, 1)), d_latent, d_key_rope.T,
                dk.reshape(LAT, HEADS, NOPE), dv.reshape(LAT, HEADS, NOPE))

    return jax.shard_map(local_step, mesh=mesh,
                         in_specs=(seq_spec, seq_spec, seq_spec, P(), P(), seq_spec),
                         out_specs=(seq_spec, seq_spec, seq_spec, seq_spec, P(), P()),
                         check_vma=False)
```

time: 160 us -> 138 us (0.86)
  Pallas kernels: 156 us -> 137 us
  local copies, waits for them, and re-layouts: 2.47 us -> 0 us
    pallas_call x1, Pallas kernels: 146 us -> 129 us  [local_step(): pl.pallas_call(attn_kernel, out_shape=(jax.ShapeDtypeStruct((HEADS, TOK,...]
    unnamed x9 -> x0, local copies, waits for them, and re-layouts: 2.47 us -> none
    pallas_call x1, Pallas kernels: 9.91 us -> 7.56 us  [to_output_layout(): pl.pallas_call(layout_kernel, grid=(PARTS,), out_shape=(jax.ShapeDtypeStr...]
where the time goes in v4:
time: 138 us; the launch traced here: 137 us
  Pallas kernels  137 us (99%)
    pallas_call x1, Pallas kernels, local_step(): pl.pallas_call(attn_kernel, out_shape=(jax.ShapeDtypeStruct((HEADS, TOK,...  129 us
    pallas_call x1, Pallas kernels, to_output_layout(): pl.pallas_call(layout_kernel, grid=(PARTS,), out_shape=(jax.ShapeDtypeStr...  7.56 us

profile of v4, /device:TPU:0, one launch (start us, length us, event | category | flops | bytes accessed | tf_op | source)
XLA Modules:
  0.0 137.5 jit_solution(9536910653666572340)
XLA Ops:
  0.6 129.3 %shard_map.109 = (bf16[16,256,128]{2,1,0:T(8,128)(2,1)}, bf16[16,192,256]{2,1,0:T(8,128)(2,1)}, f32[16,512,256]{2,1,0:T(8,128)}, bf16[256,512]{1,0:T(8,128)(2,1)}, bf16[64,256]{1,0:T(8,128)(2,1)}) custom-call(bf16[16,192,256]{2,1,0:T(8,128)(2,1)} %bitcast.10, bf16[4096,128]{1,0:T(8,128)(2,1)} %bitcast.12, bf16[256,512]{1,0:T(8,128)(2,1)} %c_in.1, ...), custom_call_target="tpu_custom_call" | custom-call | flops 30000001024 | bytes 20971520 | tf_op jit(solution)/shard_map/pallas_call | solution.py:512
  129.9 7.6 %shard_map.110 = (bf16[4096,128]{1,0:T(8,128)(2,1)}, f32[8192,128]{1,0:T(8,128)}, f32[8192,128]{1,0:T(8,128)}, bf16[16,192,256]{2,1,0:T(8,128)(2,1)}, bf16[256,512]{1,0:T(8,128)(2,1)}, /*index=5*/bf16[64,256]{1,0:T(8,128)(2,1)}) custom-call(bf16[16,256,128]{2,1,0:T(8,128)(2,1)} %get-tuple-element.17.o_t, f32[16,512,256]{2,1,0:T(8,128)} %get-tuple-element.18.dw, ...), custom_call_target="tpu_custom_call" | custom-call | tf_op jit(solution)/shard_map/pallas_call | solution.py:486

commit v5 on v4

--- a/solution.py
+++ b/solution.py
@@ -360,57 +360,65 @@
     half_x = rcopy(msg.at[0, halves[0]], rbh, d2s.at[2, 0], d2r.at[2, 0], xn)
     half_y = rcopy(msg.at[0, halves[1]], rbh, d2s.at[2, 1], d2r.at[2, 0], yn)
 
+    def on(k):
+        return pl.when(chip == k)
+
     stage3(NS - 2)
     join(0)
+    join(1)
     stage2(NS - 1)
 
-    @pl.when(chip == 3)
+    @on(3)
     def _():
         half_x.start()
         half_y.start()
-    join(1)
-
-    @pl.when(chip == 2)
-    def _():
-        for cp in to_x(1):
-            cp.start()
+
+    @on(2)
+    def _():
+        to_x(1)[0].start()
     stage5(NS - 3)
-
-    @pl.when(y == 1)
-    def _():
-        join(2)
     stage4(NS - 2)
     stage3(NS - 1)
 
-    @pl.when(chip == 2)
-    def _():
+    @pl.when(y == 1)
+    def _():
+        join(2)
+
+    @on(3)
+    def _():
+        to_x(2)[0].start()
+        to_x(1)[0].wait_recv()
+        msg[1, halves[0]] += rbx[halves[0]]
+        to_y(1)[0].start()
+
+    @on(2)
+    def _():
+        to_x(1)[1].start()
+        to_y(0)[1].start()
         half_x.wait_recv()
         msg[0, halves[0]] += rbh[...]
 
-    @pl.when(chip == 1)
-    def _():
+    @on(1)
+    def _():
+        to_x(0)[0].start()
         half_y.wait_recv()
         msg[0, halves[1]] += rbh[...]
     stage4(NS - 1)
 
-    @pl.when(chip == 1)
-    def _():
-        for cp in to_x(0):
-            cp.start()
-
-    @pl.when(chip == 2)
-    def _():
-        for cp in to_y(0):
-            cp.start()
-
-    @pl.when(chip == 3)
-    def _():
-        for cp in to_x(2):
-            cp.start()
-        for i, h in enumerate(halves):
-            to_x(1)[i].wait_recv()
-            msg[1, h] += rbx[h]
-            to_y(1)[i].start()
+    @on(3)
+    def _():
+        to_x(2)[1].start()
+        to_x(1)[1].wait_recv()
+        msg[1, halves[1]] += rbx[halves[1]]
+        to_y(1)[1].start()
+
+    @on(2)
+    def _():
+        to_y(0)[0].start()
+
+    @on(1)
+    def _():
+        to_x(0)[1].start()
 
     @pl.when(y == 1)
     def _():

time: 138 us -> 130 us (0.942)
  the two profiles are of different devices: /device:TPU:0 before, /device:TPU:2 now
where the time goes in v5:
time: 130 us
  Pallas kernels  129 us (99%)
    pallas_call x1, Pallas kernels, local_step(): pl.pallas_call(attn_kernel, out_shape=(jax.ShapeDtypeStruct((HEADS, TOK,...  122 us
    pallas_call x1, Pallas kernels, to_output_layout(): pl.pallas_call(layout_kernel, grid=(PARTS,), out_shape=(jax.ShapeDtypeStr...  7.56 us

profile of v5, /device:TPU:2, one launch (start us, length us, event | category | flops | bytes accessed | tf_op | source)
XLA Modules:
  0.0 129.9 jit_solution(18237935488232576173)
XLA Ops:
  0.6 121.7 %shard_map.109 = (bf16[16,256,128]{2,1,0:T(8,128)(2,1)}, bf16[16,192,256]{2,1,0:T(8,128)(2,1)}, f32[16,512,256]{2,1,0:T(8,128)}, bf16[256,512]{1,0:T(8,128)(2,1)}, bf16[64,256]{1,0:T(8,128)(2,1)}) custom-call(bf16[16,192,256]{2,1,0:T(8,128)(2,1)} %bitcast.10, bf16[4096,128]{1,0:T(8,128)(2,1)} %bitcast.12, bf16[256,512]{1,0:T(8,128)(2,1)} %c_in.1, ...), custom_call_target="tpu_custom_call" | custom-call | flops 30000001024 | bytes 20971520 | tf_op jit(solution)/shard_map/pallas_call | solution.py:520
  122.3 7.6 %shard_map.110 = (bf16[4096,128]{1,0:T(8,128)(2,1)}, f32[8192,128]{1,0:T(8,128)}, f32[8192,128]{1,0:T(8,128)}, bf16[16,192,256]{2,1,0:T(8,128)(2,1)}, bf16[256,512]{1,0:T(8,128)(2,1)}, /*index=5*/bf16[64,256]{1,0:T(8,128)(2,1)}) custom-call(bf16[16,256,128]{2,1,0:T(8,128)(2,1)} %get-tuple-element.17.o_t, f32[16,512,256]{2,1,0:T(8,128)} %get-tuple-element.18.dw, ...), custom_call_target="tpu_custom_call" | custom-call | tf_op jit(solution)/shard_map/pallas_call | solution.py:494

commit v6 on v5

--- a/solution.py
+++ b/solution.py
@@ -45,9 +45,9 @@
 def attn_kernel(q_in, do_in, c_in, r_in, wk_in, wv_in,
                 o_out, dq_out, dw_out, dlat_out, dr_out,
                 do_raw, wk_raw, wv_raw, stage, do_snd,
-                qt, do_ref, c_ref, rt, rn, wk, wv, o_ref, dq_ref, dw_ref, dwo, dcr, drr, msg,
+                qt, do_ref, c_ref, rt, rn, wk, wv, o_ref, dq_ref, dw_ref, dcr, drr, msg,
                 ct, kv, qn, dot_, s_buf, p_buf, rb1, rb2, rbd, rbr, rbx, rby, rbh,
-                lsem, xs, xr, cs, crs, ws, wr, fs, fr, fl, d1s, d1r, d2s, d2r):
+                lsem, xs, xr, cs, crs, ws, wr, fs, fr, d1s, d1r, d2s, d2r):
     scale = 1.0 / math.sqrt(QK)
     c2 = scale * math.log2(math.e)
     me = lax.axis_index("cp")
@@ -172,16 +172,17 @@
 
     def w_copy(phase, s):
         par = lax.rem(s, 2)
+        t = core * NS + s
         if phase == 1:
             pair = ((dw_ref.at[s, hx1, A_COLS], rb1.at[par, 0], xn), (dw_ref.at[s, hy1, B_COLS], rb1.at[par, 1], yn))
         elif phase == 2:
             pair = ((dw_ref.at[s, qa1, A_COLS], rb2.at[par, 0], yn), (dw_ref.at[s, qb1, B_COLS], rb2.at[par, 1], xn))
         elif phase == 3:
-            pair = ((dwo.at[s, qa, A_COLS], dwo.at[s, qa, A_COLS], yn),
-                    (dwo.at[s, qb, B_COLS], dwo.at[s, qb, B_COLS], xn))
+            pair = ((dw_out.at[t, qa, A_COLS], dw_out.at[t, qa, A_COLS], yn),
+                    (dw_out.at[t, qb, B_COLS], dw_out.at[t, qb, B_COLS], xn))
         else:
-            pair = ((dwo.at[s, hx, A_COLS], dwo.at[s, hx, A_COLS], xn),
-                    (dwo.at[s, hy, B_COLS], dwo.at[s, hy, B_COLS], yn))
+            pair = ((dw_out.at[t, hx, A_COLS], dw_out.at[t, hx, A_COLS], xn),
+                    (dw_out.at[t, hy, B_COLS], dw_out.at[t, hy, B_COLS], yn))
         return [rcopy(a, b, ws.at[phase - 1, par, i], wr.at[phase - 1, par, i], d)
                 for i, (a, b, d) in enumerate(pair)]
 
@@ -194,13 +195,10 @@
             cp.wait()
 
     def w_final(s, late):
-        slot = core * NS + s
+        t = core * NS + s
         parts = ((hx1, A_COLS), (hy1, B_COLS)) if late else ((hx, A_COLS), (hy, B_COLS))
-        return [rcopy(dwo.at[s, r, c], dw_out.at[slot, r, c], fs.at[s, 2 * late + i], fr.at[s, 2 * late + i], partner)
+        return [rcopy(dw_out.at[t, r, c], dw_out.at[t, r, c], fs.at[s, 2 * late + i], fr.at[s, 2 * late + i], partner)
                 for i, (r, c) in enumerate(parts)]
-
-    def w_local(s):
-        return pltpu.make_async_copy(dwo.at[s], dw_out.at[core * NS + s], fl.at[s])
 
     def stage2(s):
         par = lax.rem(s, 2)
@@ -212,8 +210,9 @@
     def stage3(s):
         par = lax.rem(s, 2)
         w_wait(2, s)
-        dwo[s, qa, A_COLS] = dw_ref[s, qa, A_COLS] + rb2[par, 0]
-        dwo[s, qb, B_COLS] = dw_ref[s, qb, B_COLS] + rb2[par, 1]
+        t = core * NS + s
+        dw_out[t, qa, A_COLS] = dw_ref[s, qa, A_COLS] + rb2[par, 0]
+        dw_out[t, qb, B_COLS] = dw_ref[s, qb, B_COLS] + rb2[par, 1]
         w_start(3, s)
 
     def stage4(s):
@@ -226,7 +225,6 @@
         w_wait(4, s)
         for cp in w_final(s, 1):
             cp.start()
-        w_local(s).start()
 
     def d1_copies(j):
         rows = pl.ds(pl.multiple_of(j * CH + (1 - core) * TOK, TOK), TOK)
@@ -333,9 +331,7 @@
     def _():
         wait_latents((2, 3))
 
-    outs = [pltpu.make_async_copy(o_ref.at[:, own_rows], o_out.at[mine], lsem.at[6]),
-            pltpu.make_async_copy(dq_ref.at[:, :, own_rows], dq_out.at[mine], lsem.at[7]),
-            rcopy(o_ref.at[:, oth_rows], o_out.at[mine], xs.at[2], xr.at[2], partner),
+    outs = [rcopy(o_ref.at[:, oth_rows], o_out.at[mine], xs.at[2], xr.at[2], partner),
             rcopy(dq_ref.at[:, :, oth_rows], dq_out.at[mine], xs.at[3], xr.at[3], partner)]
     for cp in outs:
         cp.start()
@@ -423,6 +419,12 @@
     @pl.when(y == 1)
     def _():
         join(3)
+
+    def keep(h, _):
+        o_out[core * HPC + h] = o_ref[h, own_rows, :]
+        dq_out[core * HPC + h] = dq_ref[h, :, own_rows]
+        return 0
+    lax.fori_loop(0, HPC, keep, 0)
     stage5(NS - 2)
     stage5(NS - 1)
 
@@ -466,47 +468,64 @@
     def drain(s, _):
         for cp in w_final(s, 0) + w_final(s, 1):
             cp.wait()
-        w_local(s).wait()
         return 0
     lax.fori_loop(0, NS, drain, 0)
 
 
-PARTS = 2
-
-
-def layout_kernel(o_t, dw, dq_t, dc, dr, o_ref, dk_ref, dv_ref, dq_ref, dc_ref, dr_ref):
+PARTS = 8
+
+
+def layout_kernel(dw, o_t, dq_t, dc, dr, o_out, dk_out, dv_out, dq_out, dc_out, dr_out,
+                  o_stage, stage, osem, ssem):
+    lat = LAT // PARTS
+    stores = [pltpu.make_async_copy(a, b, osem.at[i])
+              for i, (a, b) in enumerate(((o_stage, o_out), (dq_t, dq_out), (dc, dc_out), (dr, dr_out)))]
+
     def by_row(v):
         return jnp.swapaxes(v, 0, 1).reshape(v.shape[0] * v.shape[1], NOPE)
 
-    dk_ref[...] = by_row(dw[:, :, :NOPE])
-    dv_ref[...] = by_row(dw[:, :, NOPE:])
-    o_ref[...] = by_row(o_t[...].astype(F32)).astype(BF16)
-    dq_ref[...] = dq_t[...]
-    dc_ref[...] = dc[...]
-    dr_ref[...] = dr[...]
-
-
-def to_output_layout(o_t, dw, dq_t, dc, dr):
-    tok, lat = TOK // PARTS, LAT // PARTS
-    passed = [pl.BlockSpec((HEADS // PARTS, QK, TOK), lambda i: (i, 0, 0)),
-              pl.BlockSpec((tok, LAT), lambda i: (i, 0)),
-              pl.BlockSpec((ROPE // PARTS, TOK), lambda i: (i, 0))]
+    def put(i):
+        rows = pl.ds(i * lat * HEADS, lat * HEADS)
+        return [pltpu.make_async_copy(stage.at[i % 2, a], out.at[rows], ssem.at[i % 2, a])
+                for a, out in enumerate((dk_out, dv_out))]
+
+    for i in range(PARTS):
+        for a in range(2):
+            if i > 1:
+                put(i - 2)[a].wait()
+            stage[i % 2, a] = by_row(dw[:, i * lat:(i + 1) * lat, a * NOPE:(a + 1) * NOPE])
+            put(i)[a].start()
+        if i == 0:
+            for cp in stores[1:]:
+                cp.start()
+            o_stage[...] = by_row(o_t[...].astype(F32)).astype(BF16)
+            stores[0].start()
+    for i in (PARTS - 2, PARTS - 1):
+        for cp in put(i):
+            cp.wait()
+    for cp in stores:
+        cp.wait()
+
+
+def to_output_layout(dw, o_t, dq_t, dc, dr):
+    any_spec = pl.BlockSpec(memory_space=pl.ANY)
+    dma = pltpu.SemaphoreType.DMA
+    rows = LAT // PARTS * HEADS
     return pl.pallas_call(
         layout_kernel,
-        grid=(PARTS,),
         out_shape=(jax.ShapeDtypeStruct((TOK * HEADS, NOPE), BF16),
                    jax.ShapeDtypeStruct((LAT * HEADS, NOPE), F32),
                    jax.ShapeDtypeStruct((LAT * HEADS, NOPE), F32),
                    jax.ShapeDtypeStruct(dq_t.shape, BF16),
                    jax.ShapeDtypeStruct(dc.shape, BF16),
                    jax.ShapeDtypeStruct(dr.shape, BF16)),
-        in_specs=[pl.BlockSpec((HEADS, tok, NOPE), lambda i: (0, i, 0)),
-                  pl.BlockSpec((HEADS, lat, 2 * NOPE), lambda i: (0, i, 0))] + passed,
-        out_specs=[pl.BlockSpec((tok * HEADS, NOPE), lambda i: (i, 0)),
-                   pl.BlockSpec((lat * HEADS, NOPE), lambda i: (i, 0)),
-                   pl.BlockSpec((lat * HEADS, NOPE), lambda i: (i, 0))] + passed,
-        compiler_params=pltpu.CompilerParams(vmem_limit_bytes=60 << 20),
-    )(o_t, dw, dq_t, dc, dr)
+        in_specs=[pl.BlockSpec(memory_space=pltpu.VMEM)] * 5,
+        out_specs=[any_spec] * 6,
+        scratch_shapes=[pltpu.VMEM((TOK * HEADS, NOPE), BF16),
+                        pltpu.VMEM((2, 2, rows, NOPE), F32),
+                        dma((4,)), dma((2, 2))],
+        compiler_params=pltpu.CompilerParams(vmem_limit_bytes=32 << 20),
+    )(dw, o_t, dq_t, dc, dr)
 
 
 def solution(mesh):
@@ -519,13 +538,10 @@
         vm = pltpu.VMEM
         o_t, dq_t, dw, d_latent, d_key_rope = pl.pallas_call(
             attn_kernel,
-            out_shape=(jax.ShapeDtypeStruct((HEADS, TOK, NOPE), BF16),
-                       jax.ShapeDtypeStruct((HEADS, QK, TOK), BF16),
-                       jax.ShapeDtypeStruct((HEADS, LAT, 2 * NOPE), F32),
-                       jax.ShapeDtypeStruct((TOK, LAT), BF16),
-                       jax.ShapeDtypeStruct((ROPE, TOK), BF16)),
+            out_shape=(vm((HEADS, TOK, NOPE), BF16), vm((HEADS, QK, TOK), BF16), vm((HEADS, LAT, 2 * NOPE), F32),
+                       vm((TOK, LAT), BF16), vm((ROPE, TOK), BF16)),
             in_specs=[any_spec] * 6,
-            out_specs=[any_spec] * 3 + [vm_spec] * 2,
+            out_specs=[vm_spec] * 5,
             scratch_shapes=[vm((TOK * HEADS, NOPE), BF16),
                             vm((LAT, HPC, NOPE), BF16), vm((LAT, HPC, NOPE), BF16),
                             vm((TOK * HEADS, NOPE), F32), vm((HPC, TOK, NOPE), BF16),
@@ -533,7 +549,7 @@
                             vm((SEQ, LAT), BF16), vm((ROPE, SEQ), BF16), vm((SEQ, ROPE), BF16),
                             vm((HPC, LAT, NOPE), BF16), vm((HPC, LAT, NOPE), BF16),
                             vm((HPC, CH, NOPE), BF16), vm((HPC, QK, CH), BF16),
-                            vm((NS, LAT, 2 * NOPE), F32), vm((NS, LAT, 2 * NOPE), F32),
+                            vm((NS, LAT, 2 * NOPE), F32),
                             vm((SEQ, LAT), F32), vm((SEQ, ROPE), F32), vm((NCHIP, MSG, LAT), F32),
                             vm((SEQ // KC, LAT, KC), BF16), vm((SEQ, 2 * NOPE), BF16),
                             vm((CH, QK), BF16), vm((NOPE, CH), BF16),
@@ -541,14 +557,14 @@
                             vm((2, 2, 256, NOPE), F32), vm((2, 2, 128, NOPE), F32),
                             vm((NCHIP, TOK, LAT), F32), vm((NCHIP, TOK, ROPE), F32),
                             vm((MSG, LAT), F32), vm((MSG, LAT), F32), vm((MSG // 2, LAT), F32),
-                            dma((8,)), dma((4,)), dma((4,)), dma((2, 7)), dma((2, 7)),
-                            dma((4, 2, 2)), dma((4, 2, 2)), dma((NS, 4)), dma((NS, 4)), dma((NS,)),
+                            dma((6,)), dma((4,)), dma((4,)), dma((2, 7)), dma((2, 7)),
+                            dma((4, 2, 2)), dma((4, 2, 2)), dma((NS, 4)), dma((NS, 4)),
                             dma((2, NCHIP)), dma((2, NCHIP)), dma((3, 2)), dma((3, 2))],
-            compiler_params=pltpu.CompilerParams(vmem_limit_bytes=63 << 20, collective_id=0, has_side_effects=True),
+            compiler_params=pltpu.CompilerParams(vmem_limit_bytes=50 << 20, collective_id=0, has_side_effects=True),
             cost_estimate=pl.CostEstimate(flops=30 * 10**9, bytes_accessed=20 << 20, transcendentals=10**7),
         )(jnp.transpose(queries, (1, 2, 0)), d_out.reshape(TOK * HEADS, NOPE), latent, key_rope.T, w_uk, w_uv)
 
-        o, dk, dv, dq_t, d_latent, d_key_rope = to_output_layout(o_t, dw, dq_t, d_latent, d_key_rope)
+        o, dk, dv, dq_t, d_latent, d_key_rope = to_output_layout(dw, o_t, dq_t, d_latent, d_key_rope)
         return (o.reshape(TOK, HEADS, NOPE), jnp.transpose(dq_t, (2, 0, 1)), d_latent, d_key_rope.T,
                 dk.reshape(LAT, HEADS, NOPE), dv.reshape(LAT, HEADS, NOPE))
 

time: 130 us -> 127 us (0.977)
  Pallas kernels: 129 us -> 126 us
    pallas_call x2, Pallas kernels: 129 us -> 126 us  [the longest x1 121 us: local_step(): pl.pallas_call(attn_kernel, out_shape=(vm((HEADS, TOK, NOPE), BF16), vm((...]
where the time goes in v6:
time: 127 us; the launch traced here: 126 us
  Pallas kernels  126 us (99%)
    pallas_call x1, Pallas kernels, local_step(): pl.pallas_call(attn_kernel, out_shape=(vm((HEADS, TOK, NOPE), BF16), vm((...  121 us
    pallas_call x1, Pallas kernels, to_output_layout(): pl.pallas_call(layout_kernel, out_shape=(jax.ShapeDtypeStruct((TOK * HEAD...  5.01 us

profile of v6, /device:TPU:2, one launch (start us, length us, event | category | flops | bytes accessed | tf_op | source)
XLA Modules:
  0.0 126.5 jit_solution(2940482673749011516)
XLA Ops:
  0.6 120.8 %shard_map.109 = (bf16[16,256,128]{2,1,0:T(8,128)(2,1)S(1)}, bf16[16,192,256]{2,1,0:T(8,128)(2,1)S(1)}, f32[16,512,256]{2,1,0:T(8,128)S(1)}, bf16[256,512]{1,0:T(8,128)(2,1)S(1)}, bf16[64,256]{1,0:T(8,128)(2,1)S(1)}) custom-call(bf16[16,192,256]{2,1,0:T(8,128)(2,1)} %bitcast.10, bf16[4096,128]{1,0:T(8,128)(2,1)} %bitcast.12, bf16[256,512]{1,0:T(8,128)(2,1)} %c_in.1, ...), custom_call_target="tpu_custom_call" | custom-call | flops 30000001024 | bytes 20971520 | tf_op jit(solution)/shard_map/pallas_call | solution.py:539
  121.5 5.0 %shard_map.110 = (bf16[4096,128]{1,0:T(8,128)(2,1)}, f32[8192,128]{1,0:T(8,128)}, f32[8192,128]{1,0:T(8,128)}, bf16[16,192,256]{2,1,0:T(8,128)(2,1)}, bf16[256,512]{1,0:T(8,128)(2,1)}, /*index=5*/bf16[64,256]{1,0:T(8,128)(2,1)}) custom-call(f32[16,512,256]{2,1,0:T(8,128)S(1)} %get-tuple-element.17.dw, bf16[16,256,128]{2,1,0:T(8,128)(2,1)S(1)} %get-tuple-element.18.o_t, ...), custom_call_target="tpu_custom_call" | custom-call | tf_op jit(solution)/shard_map/pallas_call | solution.py:514

commit v7 on v6

--- a/solution.py
+++ b/solution.py
@@ -1,3 +1,4 @@
+import functools
 import math
 import jax
 import jax.numpy as jnp
@@ -11,6 +12,8 @@
 TOK = 256
 CH = 512
 KC = 1024
+HALF = TOK // 2
+SUB = 256
 HEADS = 16
 HPC = 8
 NS = HPC
@@ -22,8 +25,6 @@
 NCHIP = 4
 SEQ = CH * NCHIP
 MESH = pl.DeviceIdType.MESH
-A_COLS = pl.ds(0, NOPE)
-B_COLS = pl.ds(NOPE, NOPE)
 
 
 def nt(a, b):
@@ -46,8 +47,8 @@
                 o_out, dq_out, dw_out, dlat_out, dr_out,
                 do_raw, wk_raw, wv_raw, stage, do_snd,
                 qt, do_ref, c_ref, rt, rn, wk, wv, o_ref, dq_ref, dw_ref, dcr, drr, msg,
-                ct, kv, qn, dot_, s_buf, p_buf, rb1, rb2, rbd, rbr, rbx, rby, rbh,
-                lsem, xs, xr, cs, crs, ws, wr, fs, fr, d1s, d1r, d2s, d2r):
+                ct, kv, qn, dot_, s_buf, m_buf, p_buf, rb1, rb2, rbd, rbr, rbx, rby, rbh,
+                lsem, xs, xr, cs, crs, ws, wr, ps, fs, fr, d1s, d1r, d2s, d2r):
     scale = 1.0 / math.sqrt(QK)
     c2 = scale * math.log2(math.e)
     me = lax.axis_index("cp")
@@ -88,15 +89,29 @@
     local[0].wait()
     local[1].wait()
 
-    def latent_copies(i, src, dev):
+    def latent_copies(i, src, dev, recv=None):
+        recv = i if recv is None else recv
         rows = pl.ds(mul(src, TOK), TOK)
-        return (rcopy(c_ref.at[rows], c_ref.at[rows], cs.at[0, i], crs.at[0, i], dev),
-                rcopy(rt.at[:, rows], rt.at[:, rows], cs.at[1, i], crs.at[1, i], dev))
-
+        parts = [c_ref.at[pl.ds(pl.multiple_of(src * TOK + t * HALF, HALF), HALF)] for t in range(2)]
+        parts.append(rt.at[:, rows])
+        return [rcopy(ref, ref, cs.at[t, i], crs.at[t, recv], dev) for t, ref in enumerate(parts)]
+
+    low = y == 0
+    is0 = core == 0
     c_direct = [latent_copies(i, me, dev) for i, dev in enumerate((partner, xn, yn, dn))]
-    for pair in c_direct:
-        for cp in pair:
+    c_relay = latent_copies(7, yn, xn, 3)
+    for cp in c_direct[0] + c_direct[1]:
+        cp.start()
+
+    @pl.when(low)
+    def _():
+        for cp in c_direct[2]:
             cp.start()
+
+        @pl.when(is0)
+        def _():
+            for cp in c_direct[3]:
+                cp.start()
 
     heads = [rcopy(q_in.at[other], qt.at[:, :, own_rows], xs.at[0], xr.at[0], partner),
              rcopy(do_snd, do_ref.at[:, own_rows], xs.at[1], xr.at[1], partner)]
@@ -111,7 +126,6 @@
         stage[rows, :] = do_raw[rows, :].astype(F32)
         return 0
     lax.fori_loop(0, TOK * HEADS // 256, widen, 0)
-    is0 = core == 0
     for i in range(HPC):
         lo = pick(i, TOK, HEADS)
         hi = pick(i + HPC, TOK, HEADS)
@@ -148,18 +162,34 @@
 
     c_fwd = [None] + [latent_copies(3 + i, src, partner) for i, src in ((1, xn), (2, yn), (3, dn))]
 
-    def wait_latents(which):
-        for i in which:
-            for cp in c_direct[i]:
-                cp.wait()
-            for cp in c_fwd[i]:
-                cp.start()
-        for i in which:
-            for cp in c_fwd[i]:
-                cp.wait()
-
-    wait_latents((1,))
+    high = y == 1
+    for t in (0, 1, 2):
+        c_direct[1][t].wait()
+        c_fwd[1][t].start()
+
+        @pl.when(high)
+        def _(t=t):
+            c_direct[2][t].wait_recv()
+
+            @pl.when(core == 1)
+            def _():
+                c_relay[t].start()
+            c_fwd[2][t].start()
+    for cp in c_fwd[1]:
+        cp.wait()
     turn(y)
+
+    def wait_latents():
+        for t in (0, 1, 2):
+            c_direct[3][t].wait_recv()
+            c_fwd[3][t].start()
+        for cp in c_fwd[2] + c_fwd[3]:
+            cp.wait()
+
+        @pl.when(core == 1)
+        def _():
+            for cp in c_relay:
+                cp.wait_send()
 
     hx = pl.ds(mul(x, 256), 256)
     hx1 = pl.ds(mul(1 - x, 256), 256)
@@ -174,15 +204,15 @@
         par = lax.rem(s, 2)
         t = core * NS + s
         if phase == 1:
-            pair = ((dw_ref.at[s, hx1, A_COLS], rb1.at[par, 0], xn), (dw_ref.at[s, hy1, B_COLS], rb1.at[par, 1], yn))
+            pair = ((dw_ref.at[s, 0, hx1], rb1.at[par, 0], xn), (dw_ref.at[s, 1, hy1], rb1.at[par, 1], yn))
         elif phase == 2:
-            pair = ((dw_ref.at[s, qa1, A_COLS], rb2.at[par, 0], yn), (dw_ref.at[s, qb1, B_COLS], rb2.at[par, 1], xn))
+            pair = ((dw_ref.at[s, 0, qa1], rb2.at[par, 0], yn), (dw_ref.at[s, 1, qb1], rb2.at[par, 1], xn))
         elif phase == 3:
-            pair = ((dw_out.at[t, qa, A_COLS], dw_out.at[t, qa, A_COLS], yn),
-                    (dw_out.at[t, qb, B_COLS], dw_out.at[t, qb, B_COLS], xn))
+            pair = ((dw_out.at[t, 0, qa], dw_out.at[t, 0, qa], yn),
+                    (dw_out.at[t, 1, qb], dw_out.at[t, 1, qb], xn))
         else:
-            pair = ((dw_out.at[t, hx, A_COLS], dw_out.at[t, hx, A_COLS], xn),
-                    (dw_out.at[t, hy, B_COLS], dw_out.at[t, hy, B_COLS], yn))
+            pair = ((dw_out.at[t, 0, hx], dw_out.at[t, 0, hx], xn),
+                    (dw_out.at[t, 1, hy], dw_out.at[t, 1, hy], yn))
         return [rcopy(a, b, ws.at[phase - 1, par, i], wr.at[phase - 1, par, i], d)
                 for i, (a, b, d) in enumerate(pair)]
 
@@ -196,35 +226,93 @@
 
     def w_final(s, late):
         t = core * NS + s
-        parts = ((hx1, A_COLS), (hy1, B_COLS)) if late else ((hx, A_COLS), (hy, B_COLS))
-        return [rcopy(dw_out.at[t, r, c], dw_out.at[t, r, c], fs.at[s, 2 * late + i], fr.at[s, 2 * late + i], partner)
-                for i, (r, c) in enumerate(parts)]
+        par = lax.rem(s, 2)
+        parts = (hx1, hy1) if late else (hx, hy)
+        return [rcopy(dw_out.at[t, i, r], dw_out.at[t, i, r], fs.at[par, 2 * late + i], fr.at[par, 2 * late + i],
+                      partner) for i, r in enumerate(parts)]
+
+    def hand_over(s, late):
+        def wait_last():
+            for cp in w_final(s - 1, late):
+                cp.wait()
+        if isinstance(s, int):
+            wait_last()
+        else:
+            pl.when(s > 0)(wait_last)
+        for cp in w_final(s, late):
+            cp.start()
 
     def stage2(s):
         par = lax.rem(s, 2)
         w_wait(1, s)
-        dw_ref[s, hx, A_COLS] += rb1[par, 0]
-        dw_ref[s, hy, B_COLS] += rb1[par, 1]
+        dw_ref[s, 0, hx] += rb1[par, 0]
+        dw_ref[s, 1, hy] += rb1[par, 1]
         w_start(2, s)
 
     def stage3(s):
         par = lax.rem(s, 2)
         w_wait(2, s)
         t = core * NS + s
-        dw_out[t, qa, A_COLS] = dw_ref[s, qa, A_COLS] + rb2[par, 0]
-        dw_out[t, qb, B_COLS] = dw_ref[s, qb, B_COLS] + rb2[par, 1]
+        dw_out[t, 0, qa] = dw_ref[s, 0, qa] + rb2[par, 0]
+        dw_out[t, 1, qb] = dw_ref[s, 1, qb] + rb2[par, 1]
         w_start(3, s)
 
     def stage4(s):
         w_wait(3, s)
         w_start(4, s)
-        for cp in w_final(s, 0):
-            cp.start()
+        hand_over(s, 0)
 
     def stage5(s):
         w_wait(4, s)
-        for cp in w_final(s, 1):
-            cp.start()
+        hand_over(s, 1)
+
+    def last4(s):
+        w_wait(3, s)
+        to_a, to_b = w_copy(4, s)
+
+        @pl.when(low)
+        def _():
+            to_a.start()
+
+        @pl.when(chip != 3)
+        def _():
+            to_b.start()
+        hand_over(s, 0)
+
+    def w_pass(s):
+        par = lax.rem(s, 2)
+        t = core * NS + s
+        pair = ((dw_out.at[t, 0, hx1], yn), (dw_out.at[t, 1, hy1], xn))
+        return [rcopy(ref, ref, ps.at[par, i], wr.at[3, par, i], dev) for i, (ref, dev) in enumerate(pair)]
+
+    def last5a(s):
+        w_copy(4, s)[0].wait_recv()
+
+        @pl.when(low)
+        def _():
+            w_pass(s)[0].start()
+
+    def last5b(s):
+        w_copy(4, s)[1].wait_recv()
+
+        @pl.when(chip == 0)
+        def _():
+            w_pass(s)[1].start()
+        hand_over(s, 1)
+
+    def last_sent(s):
+        @pl.when(low)
+        def _():
+            w_copy(4, s)[0].wait_send()
+            w_pass(s)[0].wait_send()
+
+        @pl.when(chip != 3)
+        def _():
+            w_copy(4, s)[1].wait_send()
+
+        @pl.when(chip == 0)
+        def _():
+            w_pass(s)[1].wait_send()
 
     def d1_copies(j):
         rows = pl.ds(pl.multiple_of(j * CH + (1 - core) * TOK, TOK), TOK)
@@ -232,32 +320,43 @@
                 rcopy(drr.at[rows], rbr.at[j], d1s.at[1, j], d1r.at[1, j], partner))
 
     def step(s, _):
-        dw_ref[s] = jnp.zeros((LAT, 2 * NOPE), F32)
+        dw_ref[s] = jnp.zeros((2, LAT, NOPE), F32)
         qn[...] = qt[s].T
         dot_[...] = do_ref[s].T
         w_s = jnp.concatenate([wk[s], wv[s]], axis=1)
 
         def phase1(j, masked):
-            rows = pl.ds(mul(j, KC), KC)
-            kvv = nn(c_ref[rows, :], w_s).astype(BF16)
-            kv[rows, :] = kvv
-            k_cat = jnp.concatenate([kvv[:, :NOPE], rn[rows, :]], axis=1)
-            s2 = nn(k_cat, qt[s]) * c2
-            if masked:
-                ki = lax.broadcasted_iota(jnp.int32, (KC, CH), 0)
-                qi = lax.broadcasted_iota(jnp.int32, (KC, CH), 1)
-                s2 = jnp.where(ki - qi <= x * CH, s2, -1e30)
-            s_buf[rows, :] = s2
-            m = jnp.max(s2, axis=0, keepdims=True)
-            return m, jnp.sum(jnp.exp2(s2 - m), axis=0, keepdims=True)
+            ms, ls = [], []
+            for t in range(KC // SUB):
+                rows = pl.ds(pl.multiple_of(j * KC + t * SUB, SUB), SUB)
+                kvv = nn(c_ref[rows, :], w_s).astype(BF16)
+                kv[rows, :] = kvv
+                k_cat = jnp.concatenate([kvv[:, :NOPE], rn[rows, :]], axis=1)
+                s2 = nn(k_cat, qt[s]) * c2
+                if masked:
+                    ki = lax.broadcasted_iota(jnp.int32, (SUB, CH), 0)
+                    qi = lax.broadcasted_iota(jnp.int32, (SUB, CH), 1)
+                    s2 = jnp.where(ki - qi <= x * CH - t * SUB, s2, -1e30 * math.log2(math.e))
+                m = jnp.max(s2, axis=0, keepdims=True)
+                e = jnp.exp2(s2 - m)
+                s_buf[rows, :] = e
+                m_buf[j * (KC // SUB) + t] = m
+                ms.append(m)
+                ls.append(jnp.sum(e, axis=0, keepdims=True))
+            top = functools.reduce(jnp.maximum, ms)
+            return top, sum(l * jnp.exp2(m - top) for m, l in zip(ms, ls))
 
         stats = phase1(y, True)
 
+        @pl.when(s > 1)
+        def _():
+            stage3(s - 2)
+
         @pl.when(s == 0)
         def _():
-            @pl.when(y == 1)
+            @pl.when(high)
             def _():
-                wait_latents((2, 3))
+                wait_latents()
                 turn(0)
 
         def more(j, st):
@@ -271,17 +370,17 @@
 
         def phase2(j, acc):
             rows = pl.ds(mul(j, KC), KC)
-            pb = jnp.exp2(s_buf[rows, :] - lse).astype(BF16)
-            p_buf[rows, :] = pb
-            return acc + tn(kv[rows, NOPE:], pb)
+            parts = []
+            for t in range(KC // SUB):
+                sub = pl.ds(pl.multiple_of(j * KC + t * SUB, SUB), SUB)
+                fac = jnp.exp2(m_buf[j * (KC // SUB) + t] - lse)
+                parts.append((s_buf[sub, :] * fac).astype(BF16))
+                p_buf[sub, :] = parts[-1]
+            return acc + tn(kv[rows, NOPE:], jnp.concatenate(parts, axis=0))
 
         ot = lax.fori_loop(0, y + 1, phase2, jnp.zeros((NOPE, CH), F32))
         delta = jnp.sum(ot * dot_[...].astype(F32), axis=0, keepdims=True)
         o_ref[s] = ot.T.astype(BF16)
-
-        @pl.when(s > 1)
-        def _():
-            stage3(s - 2)
 
         def phase3(j, acc):
             rows = pl.ds(mul(j, KC), KC)
@@ -295,7 +394,9 @@
             dkv = jnp.concatenate([dkr[:, :NOPE].astype(BF16), dv.astype(BF16)], axis=1)
             drr[rows, :] += dkr[:, NOPE:]
             dcr[rows, :] += nt(dkv, w_s)
-            dw_ref[s] += nn(ct[j], dkv)
+            dw = nn(ct[j], dkv)
+            dw_ref[s, 0] += dw[:, :NOPE]
+            dw_ref[s, 1] += dw[:, NOPE:]
             out = (acc[0] + tn(k, ds), acc[1] + nn(rt[:, rows], ds))
 
             @pl.when(s == NS - 1)
@@ -309,6 +410,10 @@
                 @pl.when(s > 0)
                 def _():
                     stage2(s - 1)
+
+                @pl.when(s > 1)
+                def _():
+                    stage4(s - 2)
             return out
 
         dqn, dqr = lax.fori_loop(0, y + 1, phase3, (jnp.zeros((NOPE, CH), F32), jnp.zeros((ROPE, CH), F32)))
@@ -316,10 +421,6 @@
         dq_ref[s, :NOPE] = (dqn * scale).astype(BF16)
         dq_ref[s, NOPE:] = (dqr * scale).astype(BF16)
 
-        @pl.when(s > 1)
-        def _():
-            stage4(s - 2)
-
         @pl.when(s > 2)
         def _():
             stage5(s - 3)
@@ -327,9 +428,15 @@
 
     lax.fori_loop(0, NS, step, 0)
 
-    @pl.when(y == 0)
-    def _():
-        wait_latents((2, 3))
+    @pl.when(low)
+    def _():
+        for cp in c_direct[2]:
+            cp.wait_send()
+
+        @pl.when(is0)
+        def _():
+            for cp in c_direct[3]:
+                cp.wait_send()
 
     outs = [rcopy(o_ref.at[:, oth_rows], o_out.at[mine], xs.at[2], xr.at[2], partner),
             rcopy(dq_ref.at[:, :, oth_rows], dq_out.at[mine], xs.at[3], xr.at[3], partner)]
@@ -345,19 +452,28 @@
         msg[j, TOK:] = jnp.concatenate([drt[:ROPE // 2], drt[ROPE // 2:]], axis=1)
 
 
-    halves = (pl.ds(0, MSG // 2), pl.ds(MSG // 2, MSG // 2))
+    quarters = [pl.ds(i * (MSG // 4), MSG // 4) for i in range(4)]
 
     def to_x(j):
-        return [rcopy(msg.at[j, h], rbx.at[h], d2s.at[0, i], d2r.at[0, i], xn) for i, h in enumerate(halves)]
+        return [rcopy(msg.at[j, h], rbx.at[h], d2s.at[0, i], d2r.at[0, i], xn) for i, h in enumerate(quarters)]
 
     def to_y(j):
-        return [rcopy(msg.at[j, h], rby.at[h], d2s.at[1, i], d2r.at[1, i], yn) for i, h in enumerate(halves)]
-
-    half_x = rcopy(msg.at[0, halves[0]], rbh, d2s.at[2, 0], d2r.at[2, 0], xn)
-    half_y = rcopy(msg.at[0, halves[1]], rbh, d2s.at[2, 1], d2r.at[2, 0], yn)
+        return [rcopy(msg.at[j, h], rby.at[h], d2s.at[1, i], d2r.at[1, i], yn) for i, h in enumerate(quarters)]
+
+    half_x = [rcopy(msg.at[0, quarters[i]], rbh.at[i], d2s.at[2, i], d2r.at[2, i], xn) for i in (0, 1)]
+    half_y = [rcopy(msg.at[0, quarters[2 + i]], rbh.at[i], d2s.at[2, 2 + i], d2r.at[2, i], yn) for i in (0, 1)]
+
+    def start(copies):
+        for cp in copies:
+            cp.start()
 
     def on(k):
         return pl.when(chip == k)
+
+    def add_and_pass(i):
+        to_x(1)[i].wait_recv()
+        msg[1, quarters[i]] += rbx[quarters[i]]
+        to_y(1)[i].start()
 
     stage3(NS - 2)
     join(0)
@@ -366,57 +482,65 @@
 
     @on(3)
     def _():
-        half_x.start()
-        half_y.start()
+        start((half_x[0], half_y[0]))
 
     @on(2)
     def _():
         to_x(1)[0].start()
     stage5(NS - 3)
-    stage4(NS - 2)
+    last4(NS - 2)
     stage3(NS - 1)
 
-    @pl.when(y == 1)
+    @pl.when(high)
     def _():
         join(2)
 
     @on(3)
     def _():
-        to_x(2)[0].start()
-        to_x(1)[0].wait_recv()
-        msg[1, halves[0]] += rbx[halves[0]]
-        to_y(1)[0].start()
+        start((half_x[1], half_y[1], to_x(2)[0]))
+        add_and_pass(0)
+        add_and_pass(1)
+        to_x(2)[1].start()
 
     @on(2)
     def _():
-        to_x(1)[1].start()
-        to_y(0)[1].start()
-        half_x.wait_recv()
-        msg[0, halves[0]] += rbh[...]
+        start(to_x(1)[1:])
+        start(to_y(0)[2:])
 
     @on(1)
     def _():
-        to_x(0)[0].start()
-        half_y.wait_recv()
-        msg[0, halves[1]] += rbh[...]
-    stage4(NS - 1)
+        start(to_x(0)[:2])
+
+    @pl.when(low)
+    def _():
+        last5a(NS - 2)
+
+    @on(0)
+    def _():
+        last5b(NS - 2)
+    last4(NS - 1)
 
     @on(3)
     def _():
-        to_x(2)[1].start()
-        to_x(1)[1].wait_recv()
-        msg[1, halves[1]] += rbx[halves[1]]
-        to_y(1)[1].start()
+        start(to_x(2)[2:])
+        add_and_pass(2)
+        add_and_pass(3)
 
     @on(2)
     def _():
-        to_y(0)[0].start()
+        for i in (0, 1):
+            half_x[i].wait_recv()
+            msg[0, quarters[i]] += rbh[i]
+            to_y(0)[i].start()
 
     @on(1)
     def _():
-        to_x(0)[1].start()
-
-    @pl.when(y == 1)
+        for i in (0, 1):
+            half_y[i].wait_recv()
+            msg[0, quarters[2 + i]] += rbh[i]
+            to_x(0)[2 + i].start()
+
+    @pl.when(high)
     def _():
         join(3)
 
@@ -425,8 +549,18 @@
         dq_out[core * HPC + h] = dq_ref[h, :, own_rows]
         return 0
     lax.fori_loop(0, HPC, keep, 0)
-    stage5(NS - 2)
-    stage5(NS - 1)
+
+    @pl.when(high)
+    def _():
+        last5a(NS - 2)
+
+    @pl.when(chip != 0)
+    def _():
+        last5b(NS - 2)
+    last5a(NS - 1)
+    last5b(NS - 1)
+    last_sent(NS - 2)
+    last_sent(NS - 1)
 
     def all_of(copies, recv):
         for cp in copies:
@@ -461,18 +595,15 @@
 
     @pl.when(chip == 3)
     def _():
-        all_of((half_x, half_y), False)
+        all_of(half_x + half_y, False)
     for cp in outs:
         cp.wait()
 
-    def drain(s, _):
-        for cp in w_final(s, 0) + w_final(s, 1):
-            cp.wait()
-        return 0
-    lax.fori_loop(0, NS, drain, 0)
-
-
-PARTS = 8
+    for cp in w_final(NS - 1, 0) + w_final(NS - 1, 1):
+        cp.wait()
+
+
+PARTS = 4
 
 
 def layout_kernel(dw, o_t, dq_t, dc, dr, o_out, dk_out, dv_out, dq_out, dc_out, dr_out,
@@ -493,7 +624,7 @@
         for a in range(2):
             if i > 1:
                 put(i - 2)[a].wait()
-            stage[i % 2, a] = by_row(dw[:, i * lat:(i + 1) * lat, a * NOPE:(a + 1) * NOPE])
+            stage[i % 2, a] = by_row(dw[:, a, i * lat:(i + 1) * lat])
             put(i)[a].start()
         if i == 0:
             for cp in stores[1:]:
@@ -538,7 +669,7 @@
         vm = pltpu.VMEM
         o_t, dq_t, dw, d_latent, d_key_rope = pl.pallas_call(
             attn_kernel,
-            out_shape=(vm((HEADS, TOK, NOPE), BF16), vm((HEADS, QK, TOK), BF16), vm((HEADS, LAT, 2 * NOPE), F32),
+            out_shape=(vm((HEADS, TOK, NOPE), BF16), vm((HEADS, QK, TOK), BF16), vm((HEADS, 2, LAT, NOPE), F32),
                        vm((TOK, LAT), BF16), vm((ROPE, TOK), BF16)),
             in_specs=[any_spec] * 6,
             out_specs=[vm_spec] * 5,
@@ -549,17 +680,17 @@
                             vm((SEQ, LAT), BF16), vm((ROPE, SEQ), BF16), vm((SEQ, ROPE), BF16),
                             vm((HPC, LAT, NOPE), BF16), vm((HPC, LAT, NOPE), BF16),
                             vm((HPC, CH, NOPE), BF16), vm((HPC, QK, CH), BF16),
-                            vm((NS, LAT, 2 * NOPE), F32),
+                            vm((NS, 2, LAT, NOPE), F32),
                             vm((SEQ, LAT), F32), vm((SEQ, ROPE), F32), vm((NCHIP, MSG, LAT), F32),
                             vm((SEQ // KC, LAT, KC), BF16), vm((SEQ, 2 * NOPE), BF16),
                             vm((CH, QK), BF16), vm((NOPE, CH), BF16),
-                            vm((SEQ, CH), F32), vm((SEQ, CH), BF16),
+                            vm((SEQ, CH), F32), vm((SEQ // SUB, 1, CH), F32), vm((SEQ, CH), BF16),
                             vm((2, 2, 256, NOPE), F32), vm((2, 2, 128, NOPE), F32),
                             vm((NCHIP, TOK, LAT), F32), vm((NCHIP, TOK, ROPE), F32),
-                            vm((MSG, LAT), F32), vm((MSG, LAT), F32), vm((MSG // 2, LAT), F32),
-                            dma((6,)), dma((4,)), dma((4,)), dma((2, 7)), dma((2, 7)),
-                            dma((4, 2, 2)), dma((4, 2, 2)), dma((NS, 4)), dma((NS, 4)),
-                            dma((2, NCHIP)), dma((2, NCHIP)), dma((3, 2)), dma((3, 2))],
+                            vm((MSG, LAT), F32), vm((MSG, LAT), F32), vm((2, MSG // 4, LAT), F32),
+                            dma((6,)), dma((4,)), dma((4,)), dma((3, 8)), dma((3, 7)),
+                            dma((4, 2, 2)), dma((4, 2, 2)), dma((2, 2)), dma((2, 4)), dma((2, 4)),
+                            dma((2, NCHIP)), dma((2, NCHIP)), dma((3, 4)), dma((3, 4))],
             compiler_params=pltpu.CompilerParams(vmem_limit_bytes=50 << 20, collective_id=0, has_side_effects=True),
             cost_estimate=pl.CostEstimate(flops=30 * 10**9, bytes_accessed=20 << 20, transcendentals=10**7),
         )(jnp.transpose(queries, (1, 2, 0)), d_out.reshape(TOK * HEADS, NOPE), latent, key_rope.T, w_uk, w_uv)

time: 127 us -> 116 us (0.913)
  the two profiles are of different devices: /device:TPU:2 before, /device:TPU:0 now
where the time goes in v7:
time: 116 us
  Pallas kernels  115 us (99%)
    pallas_call x1, Pallas kernels, local_step(): pl.pallas_call(attn_kernel, out_shape=(vm((HEADS, TOK, NOPE), BF16), vm((...  111 us
    pallas_call x1, Pallas kernels, to_output_layout(): pl.pallas_call(layout_kernel, out_shape=(jax.ShapeDtypeStruct((TOK * HEAD...  4.28 us

profile of v7, /device:TPU:0, one launch (start us, length us, event | category | flops | bytes accessed | tf_op | source)
XLA Modules:
  0.0 116.1 jit_solution(16743846842442411976)
XLA Ops:
  0.6 111.2 %shard_map.109 = (bf16[16,256,128]{2,1,0:T(8,128)(2,1)S(1)}, bf16[16,192,256]{2,1,0:T(8,128)(2,1)S(1)}, f32[16,2,512,128]{3,2,1,0:T(8,128)S(1)}, bf16[256,512]{1,0:T(8,128)(2,1)S(1)}, bf16[64,256]{1,0:T(8,128)(2,1)S(1)}) custom-call(bf16[16,192,256]{2,1,0:T(8,128)(2,1)} %bitcast.10, bf16[4096,128]{1,0:T(8,128)(2,1)} %bitcast.12, bf16[256,512]{1,0:T(8,128)(2,1)} %c_in.1, ...), custom_call_target="tpu_custom_call" | custom-call | flops 30000001024 | bytes 20971520 | tf_op jit(solution)/shard_map/pallas_call | solution.py:670
  111.8 4.3 %shard_map.110 = (bf16[4096,128]{1,0:T(8,128)(2,1)}, f32[8192,128]{1,0:T(8,128)}, f32[8192,128]{1,0:T(8,128)}, bf16[16,192,256]{2,1,0:T(8,128)(2,1)}, bf16[256,512]{1,0:T(8,128)(2,1)}, /*index=5*/bf16[64,256]{1,0:T(8,128)(2,1)}) custom-call(f32[16,2,512,128]{3,2,1,0:T(8,128)S(1)} %get-tuple-element.17.dw, bf16[16,256,128]{2,1,0:T(8,128)(2,1)S(1)} %get-tuple-element.18.o_t, ...), custom_call_target="tpu_custom_call" | custom-call | tf_op jit(solution)/shard_map/pallas_call | solution.py:645

commit v8 on v7

--- a/solution.py
+++ b/solution.py
@@ -21,7 +21,7 @@
 ROPE = 64
 QK = NOPE + ROPE
 LAT = 512
-MSG = TOK + ROPE // 2
+PACK = ROPE // 2
 NCHIP = 4
 SEQ = CH * NCHIP
 MESH = pl.DeviceIdType.MESH
@@ -46,9 +46,9 @@
 def attn_kernel(q_in, do_in, c_in, r_in, wk_in, wv_in,
                 o_out, dq_out, dw_out, dlat_out, dr_out,
                 do_raw, wk_raw, wv_raw, stage, do_snd,
-                qt, do_ref, c_ref, rt, rn, wk, wv, o_ref, dq_ref, dw_ref, dcr, drr, msg,
-                ct, kv, qn, dot_, s_buf, m_buf, p_buf, rb1, rb2, rbd, rbr, rbx, rby, rbh,
-                lsem, xs, xr, cs, crs, ws, wr, ps, fs, fr, d1s, d1r, d2s, d2r):
+                qt, do_ref, c_ref, rt, rn, wk, wv, o_ref, dq_ref, dw_ref, dcr, drr, msg, msr, mrb,
+                ct, kv, qn, dot_, s_buf, m_buf, p_buf, rb1, rb2, rbd, rbr, rbx, rby, rbh, rbxr, rbyr,
+                lsem, xs, xr, cs, crs, ws, wr, ps, fs, fr):
     scale = 1.0 / math.sqrt(QK)
     c2 = scale * math.log2(math.e)
     me = lax.axis_index("cp")
@@ -316,8 +316,8 @@
 
     def d1_copies(j):
         rows = pl.ds(pl.multiple_of(j * CH + (1 - core) * TOK, TOK), TOK)
-        return (rcopy(dcr.at[rows], rbd.at[j], d1s.at[0, j], d1r.at[0, j], partner),
-                rcopy(drr.at[rows], rbr.at[j], d1s.at[1, j], d1r.at[1, j], partner))
+        return (rcopy(dcr.at[rows], rbd.at[j], cs.at[0, j], crs.at[0, j], partner),
+                rcopy(drr.at[rows], rbr.at[j], cs.at[1, j], crs.at[1, j], partner))
 
     def step(s, _):
         dw_ref[s] = jnp.zeros((2, LAT, NOPE), F32)
@@ -359,6 +359,16 @@
                 wait_latents()
                 turn(0)
 
+            @pl.when(low)
+            def _():
+                for cp in c_direct[2]:
+                    cp.wait_send()
+
+                @pl.when(is0)
+                def _():
+                    for cp in c_direct[3]:
+                        cp.wait_send()
+
         def more(j, st):
             m0, l0 = st
             m1, l1 = phase1(j, False)
@@ -410,10 +420,6 @@
                 @pl.when(s > 0)
                 def _():
                     stage2(s - 1)
-
-                @pl.when(s > 1)
-                def _():
-                    stage4(s - 2)
             return out
 
         dqn, dqr = lax.fori_loop(0, y + 1, phase3, (jnp.zeros((NOPE, CH), F32), jnp.zeros((ROPE, CH), F32)))
@@ -421,22 +427,16 @@
         dq_ref[s, :NOPE] = (dqn * scale).astype(BF16)
         dq_ref[s, NOPE:] = (dqr * scale).astype(BF16)
 
+        @pl.when(s > 1)
+        def _():
+            stage4(s - 2)
+
         @pl.when(s > 2)
         def _():
             stage5(s - 3)
         return 0
 
     lax.fori_loop(0, NS, step, 0)
-
-    @pl.when(low)
-    def _():
-        for cp in c_direct[2]:
-            cp.wait_send()
-
-        @pl.when(is0)
-        def _():
-            for cp in c_direct[3]:
-                cp.wait_send()
 
     outs = [rcopy(o_ref.at[:, oth_rows], o_out.at[mine], xs.at[2], xr.at[2], partner),
             rcopy(dq_ref.at[:, :, oth_rows], dq_out.at[mine], xs.at[3], xr.at[3], partner)]
@@ -447,21 +447,30 @@
         for cp in d1_copies(j):
             cp.wait()
         rows = pl.ds(pl.multiple_of(j * CH + core * TOK, TOK), TOK)
-        msg[j, :TOK] = dcr[rows, :] + rbd[j]
+        msg[j] = dcr[rows, :] + rbd[j]
         drt = (drr[rows, :] + rbr[j]).T
-        msg[j, TOK:] = jnp.concatenate([drt[:ROPE // 2], drt[ROPE // 2:]], axis=1)
-
-
-    quarters = [pl.ds(i * (MSG // 4), MSG // 4) for i in range(4)]
+        msr[j] = jnp.concatenate([drt[:PACK], drt[PACK:]], axis=1)
+        mrb[j] = msr[j].astype(BF16)
+
+
+    quarters = [pl.ds(i * (TOK // 4), TOK // 4) for i in range(4)]
+
+    def slot(kind, i):
+        if kind == 2:
+            return 2, i
+        return (kind, 4 + i) if i < 4 else (2, 5 + kind)
 
     def to_x(j):
-        return [rcopy(msg.at[j, h], rbx.at[h], d2s.at[0, i], d2r.at[0, i], xn) for i, h in enumerate(quarters)]
+        return ([rcopy(msg.at[j, h], rbx.at[h], cs.at[slot(0, i)], crs.at[slot(0, i)], xn) for i, h in enumerate(quarters)]
+                + [rcopy(mrb.at[j], rbxr, cs.at[slot(0, 4)], crs.at[slot(0, 4)], xn)])
 
     def to_y(j):
-        return [rcopy(msg.at[j, h], rby.at[h], d2s.at[1, i], d2r.at[1, i], yn) for i, h in enumerate(quarters)]
-
-    half_x = [rcopy(msg.at[0, quarters[i]], rbh.at[i], d2s.at[2, i], d2r.at[2, i], xn) for i in (0, 1)]
-    half_y = [rcopy(msg.at[0, quarters[2 + i]], rbh.at[i], d2s.at[2, 2 + i], d2r.at[2, i], yn) for i in (0, 1)]
+        return ([rcopy(msg.at[j, h], rby.at[h], cs.at[slot(1, i)], crs.at[slot(1, i)], yn) for i, h in enumerate(quarters)]
+                + [rcopy(mrb.at[j], rbyr, cs.at[slot(1, 4)], crs.at[slot(1, 4)], yn)])
+
+    half_x = [rcopy(msg.at[0, quarters[i]], rbh.at[i], cs.at[slot(2, i)], crs.at[slot(2, i)], xn) for i in (0, 1)]
+    half_y = [rcopy(msg.at[0, quarters[2 + i]], rbh.at[i], cs.at[slot(2, 2 + i)], crs.at[slot(2, i)], yn) for i in (0, 1)]
+    half_y.append(rcopy(mrb.at[0], rbxr, cs.at[slot(2, 4)], crs.at[slot(2, 4)], yn))
 
     def start(copies):
         for cp in copies:
@@ -475,29 +484,34 @@
         msg[1, quarters[i]] += rbx[quarters[i]]
         to_y(1)[i].start()
 
+    def add_dr(j, buf):
+        msr[j] += buf[...].astype(F32)
+        mrb[j] = msr[j].astype(BF16)
+
     stage3(NS - 2)
     join(0)
     join(1)
     stage2(NS - 1)
 
-    @on(3)
-    def _():
-        start((half_x[0], half_y[0]))
-
-    @on(2)
-    def _():
-        to_x(1)[0].start()
     stage5(NS - 3)
     last4(NS - 2)
     stage3(NS - 1)
 
+    @on(3)
+    def _():
+        start((half_x[0], half_y[0]))
+
+    @on(2)
+    def _():
+        to_x(1)[0].start()
+
     @pl.when(high)
     def _():
         join(2)
 
     @on(3)
     def _():
-        start((half_x[1], half_y[1], to_x(2)[0]))
+        start((half_x[1], half_y[1], half_y[2], to_x(2)[0]))
         add_and_pass(0)
         add_and_pass(1)
         to_x(2)[1].start()
@@ -525,6 +539,9 @@
         start(to_x(2)[2:])
         add_and_pass(2)
         add_and_pass(3)
+        to_x(1)[4].wait_recv()
+        add_dr(1, rbxr)
+        to_y(1)[4].start()
 
     @on(2)
     def _():
@@ -539,6 +556,9 @@
             half_y[i].wait_recv()
             msg[0, quarters[2 + i]] += rbh[i]
             to_x(0)[2 + i].start()
+        half_y[2].wait_recv()
+        add_dr(0, rbxr)
+        to_x(0)[4].start()
 
     @pl.when(high)
     def _():
@@ -575,15 +595,17 @@
         def _():
             all_of(to_x(0), True)
             msg[chip] += rbx[...]
+            add_dr(chip, rbxr)
 
         @pl.when(chip != 2)
         def _():
             all_of(to_y(0), True)
             msg[chip] += rby[...]
-
-    dlat_out[...] = msg[chip, :TOK].astype(BF16)
-    dr_out[:ROPE // 2] = msg[chip, TOK:, :TOK].astype(BF16)
-    dr_out[ROPE // 2:] = msg[chip, TOK:, TOK:].astype(BF16)
+            add_dr(chip, rbyr)
+
+    dlat_out[...] = msg[chip].astype(BF16)
+    dr_out[:PACK] = msr[chip, :, :TOK].astype(BF16)
+    dr_out[PACK:] = msr[chip, :, TOK:].astype(BF16)
 
     @pl.when(chip != 0)
     def _():
@@ -681,16 +703,16 @@
                             vm((HPC, LAT, NOPE), BF16), vm((HPC, LAT, NOPE), BF16),
                             vm((HPC, CH, NOPE), BF16), vm((HPC, QK, CH), BF16),
                             vm((NS, 2, LAT, NOPE), F32),
-                            vm((SEQ, LAT), F32), vm((SEQ, ROPE), F32), vm((NCHIP, MSG, LAT), F32),
+                            vm((SEQ, LAT), F32), vm((SEQ, ROPE), F32), vm((NCHIP, TOK, LAT), F32), vm((NCHIP, PACK, LAT), F32), vm((NCHIP, PACK, LAT), BF16),
                             vm((SEQ // KC, LAT, KC), BF16), vm((SEQ, 2 * NOPE), BF16),
                             vm((CH, QK), BF16), vm((NOPE, CH), BF16),
                             vm((SEQ, CH), F32), vm((SEQ // SUB, 1, CH), F32), vm((SEQ, CH), BF16),
                             vm((2, 2, 256, NOPE), F32), vm((2, 2, 128, NOPE), F32),
                             vm((NCHIP, TOK, LAT), F32), vm((NCHIP, TOK, ROPE), F32),
-                            vm((MSG, LAT), F32), vm((MSG, LAT), F32), vm((2, MSG // 4, LAT), F32),
-                            dma((6,)), dma((4,)), dma((4,)), dma((3, 8)), dma((3, 7)),
-                            dma((4, 2, 2)), dma((4, 2, 2)), dma((2, 2)), dma((2, 4)), dma((2, 4)),
-                            dma((2, NCHIP)), dma((2, NCHIP)), dma((3, 4)), dma((3, 4))],
+                            vm((TOK, LAT), F32), vm((TOK, LAT), F32), vm((2, TOK // 4, LAT), F32),
+                            vm((PACK, LAT), BF16), vm((PACK, LAT), BF16),
+                            dma((6,)), dma((4,)), dma((4,)), dma((3, 8)), dma((3, 8)),
+                            dma((4, 2, 2)), dma((4, 2, 2)), dma((2, 2)), dma((2, 4)), dma((2, 4))],
             compiler_params=pltpu.CompilerParams(vmem_limit_bytes=50 << 20, collective_id=0, has_side_effects=True),
             cost_estimate=pl.CostEstimate(flops=30 * 10**9, bytes_accessed=20 << 20, transcendentals=10**7),
         )(jnp.transpose(queries, (1, 2, 0)), d_out.reshape(TOK * HEADS, NOPE), latent, key_rope.T, w_uk, w_uv)

time: 116 us -> 115 us (level)
  no operation moved by 1% of the time
where the time goes in v8:
time: 115 us
  Pallas kernels  114 us (99%)
    pallas_call x1, Pallas kernels, local_step(): pl.pallas_call(attn_kernel, out_shape=(vm((HEADS, TOK, NOPE), BF16), vm((...  110 us
    pallas_call x1, Pallas kernels, to_output_layout(): pl.pallas_call(layout_kernel, out_shape=(jax.ShapeDtypeStruct((TOK * HEAD...  4.28 us

profile of v8, /device:TPU:0, one launch (start us, length us, event | category | flops | bytes accessed | tf_op | source)
XLA Modules:
  0.0 115.0 jit_solution(14960916274952002896)
XLA Ops:
  0.6 110.1 %shard_map.109 = (bf16[16,256,128]{2,1,0:T(8,128)(2,1)S(1)}, bf16[16,192,256]{2,1,0:T(8,128)(2,1)S(1)}, f32[16,2,512,128]{3,2,1,0:T(8,128)S(1)}, bf16[256,512]{1,0:T(8,128)(2,1)S(1)}, bf16[64,256]{1,0:T(8,128)(2,1)S(1)}) custom-call(bf16[16,192,256]{2,1,0:T(8,128)(2,1)} %bitcast.10, bf16[4096,128]{1,0:T(8,128)(2,1)} %bitcast.12, bf16[256,512]{1,0:T(8,128)(2,1)} %c_in.1, ...), custom_call_target="tpu_custom_call" | custom-call | flops 30000001024 | bytes 20971520 | tf_op jit(solution)/shard_map/pallas_call | solution.py:692
  110.7 4.3 %shard_map.110 = (bf16[4096,128]{1,0:T(8,128)(2,1)}, f32[8192,128]{1,0:T(8,128)}, f32[8192,128]{1,0:T(8,128)}, bf16[16,192,256]{2,1,0:T(8,128)(2,1)}, bf16[256,512]{1,0:T(8,128)(2,1)}, /*index=5*/bf16[64,256]{1,0:T(8,128)(2,1)}) custom-call(f32[16,2,512,128]{3,2,1,0:T(8,128)S(1)} %get-tuple-element.17.dw, bf16[16,256,128]{2,1,0:T(8,128)(2,1)S(1)} %get-tuple-element.18.o_t, ...), custom_call_target="tpu_custom_call" | custom-call | tf_op jit(solution)/shard_map/pallas_call | solution.py:667

commit v9 on v8

--- a/solution.py
+++ b/solution.py
@@ -375,15 +375,15 @@
             m = jnp.maximum(m0, m1)
             return m, l0 * jnp.exp2(m0 - m) + l1 * jnp.exp2(m1 - m)
 
-        m, l = lax.fori_loop(0, y, more, stats)
-        lse = m + jnp.log2(l)
+        top, l = lax.fori_loop(0, y, more, stats)
+        inv = 1.0 / l
 
         def phase2(j, acc):
             rows = pl.ds(mul(j, KC), KC)
             parts = []
             for t in range(KC // SUB):
                 sub = pl.ds(pl.multiple_of(j * KC + t * SUB, SUB), SUB)
-                fac = jnp.exp2(m_buf[j * (KC // SUB) + t] - lse)
+                fac = jnp.exp2(m_buf[j * (KC // SUB) + t] - top) * inv
                 parts.append((s_buf[sub, :] * fac).astype(BF16))
                 p_buf[sub, :] = parts[-1]
             return acc + tn(kv[rows, NOPE:], jnp.concatenate(parts, axis=0))

time: 115 us -> 115 us (level)
  no operation moved by 1% of the time
where the time goes in v9:
time: 115 us
  Pallas kernels  114 us (99%)
    pallas_call x1, Pallas kernels, local_step(): pl.pallas_call(attn_kernel, out_shape=(vm((HEADS, TOK, NOPE), BF16), vm((...  110 us
    pallas_call x1, Pallas kernels, to_output_layout(): pl.pallas_call(layout_kernel, out_shape=(jax.ShapeDtypeStruct((TOK * HEAD...  4.28 us

profile of v9, /device:TPU:0, one launch (start us, length us, event | category | flops | bytes accessed | tf_op | source)
XLA Modules:
  0.0 114.9 jit_solution(13067649243456817690)
XLA Ops:
  0.6 110.0 %shard_map.109 = (bf16[16,256,128]{2,1,0:T(8,128)(2,1)S(1)}, bf16[16,192,256]{2,1,0:T(8,128)(2,1)S(1)}, f32[16,2,512,128]{3,2,1,0:T(8,128)S(1)}, bf16[256,512]{1,0:T(8,128)(2,1)S(1)}, bf16[64,256]{1,0:T(8,128)(2,1)S(1)}) custom-call(bf16[16,192,256]{2,1,0:T(8,128)(2,1)} %bitcast.10, bf16[4096,128]{1,0:T(8,128)(2,1)} %bitcast.12, bf16[256,512]{1,0:T(8,128)(2,1)} %c_in.1, ...), custom_call_target="tpu_custom_call" | custom-call | flops 30000001024 | bytes 20971520 | tf_op jit(solution)/shard_map/pallas_call | solution.py:692
  110.6 4.3 %shard_map.110 = (bf16[4096,128]{1,0:T(8,128)(2,1)}, f32[8192,128]{1,0:T(8,128)}, f32[8192,128]{1,0:T(8,128)}, bf16[16,192,256]{2,1,0:T(8,128)(2,1)}, bf16[256,512]{1,0:T(8,128)(2,1)}, /*index=5*/bf16[64,256]{1,0:T(8,128)(2,1)}) custom-call(f32[16,2,512,128]{3,2,1,0:T(8,128)S(1)} %get-tuple-element.17.dw, bf16[16,256,128]{2,1,0:T(8,128)(2,1)S(1)} %get-tuple-element.18.o_t, ...), custom_call_target="tpu_custom_call" | custom-call | tf_op jit(solution)/shard_map/pallas_call | solution.py:667

commit v10 on v9

--- a/solution.py
+++ b/solution.py
@@ -348,6 +348,10 @@
 
         stats = phase1(y, True)
 
+        @pl.when(s > 3)
+        def _():
+            stage5(s - 4)
+
         @pl.when(s > 1)
         def _():
             stage3(s - 2)
@@ -430,16 +434,12 @@
         @pl.when(s > 1)
         def _():
             stage4(s - 2)
-
-        @pl.when(s > 2)
-        def _():
-            stage5(s - 3)
         return 0
 
     lax.fori_loop(0, NS, step, 0)
 
-    outs = [rcopy(o_ref.at[:, oth_rows], o_out.at[mine], xs.at[2], xr.at[2], partner),
-            rcopy(dq_ref.at[:, :, oth_rows], dq_out.at[mine], xs.at[3], xr.at[3], partner)]
+    outs = [rcopy(o_ref.at[:, oth_rows], o_out.at[mine], xs.at[0], xr.at[0], partner),
+            rcopy(dq_ref.at[:, :, oth_rows], dq_out.at[mine], xs.at[1], xr.at[1], partner)]
     for cp in outs:
         cp.start()
 
@@ -488,6 +488,7 @@
         msr[j] += buf[...].astype(F32)
         mrb[j] = msr[j].astype(BF16)
 
+    stage5(NS - 4)
     stage3(NS - 2)
     join(0)
     join(1)
@@ -711,7 +712,7 @@
                             vm((NCHIP, TOK, LAT), F32), vm((NCHIP, TOK, ROPE), F32),
                             vm((TOK, LAT), F32), vm((TOK, LAT), F32), vm((2, TOK // 4, LAT), F32),
                             vm((PACK, LAT), BF16), vm((PACK, LAT), BF16),
-                            dma((6,)), dma((4,)), dma((4,)), dma((3, 8)), dma((3, 8)),
+                            dma((6,)), dma((2,)), dma((2,)), dma((3, 8)), dma((3, 8)),
                             dma((4, 2, 2)), dma((4, 2, 2)), dma((2, 2)), dma((2, 4)), dma((2, 4))],
             compiler_params=pltpu.CompilerParams(vmem_limit_bytes=50 << 20, collective_id=0, has_side_effects=True),
             cost_estimate=pl.CostEstimate(flops=30 * 10**9, bytes_accessed=20 << 20, transcendentals=10**7),

time: 115 us -> 115 us (level)
  no operation moved by 1% of the time
where the time goes in v10:
time: 115 us
  Pallas kernels  114 us (99%)
    pallas_call x1, Pallas kernels, local_step(): pl.pallas_call(attn_kernel, out_shape=(vm((HEADS, TOK, NOPE), BF16), vm((...  110 us
    pallas_call x1, Pallas kernels, to_output_layout(): pl.pallas_call(layout_kernel, out_shape=(jax.ShapeDtypeStruct((TOK * HEAD...  4.28 us

profile of v10, /device:TPU:0, one launch (start us, length us, event | category | flops | bytes accessed | tf_op | source)
XLA Modules:
  0.0 114.9 jit_solution(772189111877682106)
XLA Ops:
  0.6 110.0 %shard_map.109 = (bf16[16,256,128]{2,1,0:T(8,128)(2,1)S(1)}, bf16[16,192,256]{2,1,0:T(8,128)(2,1)S(1)}, f32[16,2,512,128]{3,2,1,0:T(8,128)S(1)}, bf16[256,512]{1,0:T(8,128)(2,1)S(1)}, bf16[64,256]{1,0:T(8,128)(2,1)S(1)}) custom-call(bf16[16,192,256]{2,1,0:T(8,128)(2,1)} %bitcast.10, bf16[4096,128]{1,0:T(8,128)(2,1)} %bitcast.12, bf16[256,512]{1,0:T(8,128)(2,1)} %c_in.1, ...), custom_call_target="tpu_custom_call" | custom-call | flops 30000001024 | bytes 20971520 | tf_op jit(solution)/shard_map/pallas_call | solution.py:693
  110.6 4.3 %shard_map.110 = (bf16[4096,128]{1,0:T(8,128)(2,1)}, f32[8192,128]{1,0:T(8,128)}, f32[8192,128]{1,0:T(8,128)}, bf16[16,192,256]{2,1,0:T(8,128)(2,1)}, bf16[256,512]{1,0:T(8,128)(2,1)}, /*index=5*/bf16[64,256]{1,0:T(8,128)(2,1)}) custom-call(f32[16,2,512,128]{3,2,1,0:T(8,128)S(1)} %get-tuple-element.17.dw, bf16[16,256,128]{2,1,0:T(8,128)(2,1)S(1)} %get-tuple-element.18.o_t, ...), custom_call_target="tpu_custom_call" | custom-call | tf_op jit(solution)/shard_map/pallas_call | solution.py:668
